TPU v7x, 512 devices: a 4x2x32 block of a 4x8x32 slice. The times are simulated.
512 devices in a mesh: graphs: 2 (over y), rows: 32 (over z), cols: 4 (over x), sub: 2 (over core).
Axes of the slice: x: 4, y: 2, z: 32, core: 2. Of those that a mesh axis runs over, the one named last changes fastest.
The devices are a block of a 4x8x32 slice.
Arguments:
- current_block: float32 [16, 1048576], P(None, ('graphs', 'rows', 'cols', 'sub')), parts along dimension 1, may hold values from -1200 to 1200, as said below
- previous_block: float32 [16, 1048576], P(None, ('graphs', 'rows', 'cols', 'sub')), parts along dimension 1, may hold values from -1200 to 1200, as said below
- adjacency_tiles: float32 [24576, 128, 128], P(('graphs', 'rows', 'cols', 'sub')), parts along dimension 0, may hold values from -0.3125 to 0.3125
- tile_rows: int32 [24576], P(('graphs', 'rows', 'cols', 'sub')), parts along dimension 0, may hold values from 0 to 4095, as said below
- tile_cols: int32 [24576], P(('graphs', 'rows', 'cols', 'sub')), parts along dimension 0, may hold values from 0 to 4095, as said below
- tile_count: int32 [512], P(('graphs', 'rows', 'cols', 'sub')), parts along dimension 0, may hold values from 18 to 48, as said below
- locked: int32 [2], P('graphs'), parts along dimension 0, may hold values from 0 to 7
Outputs:
- w_basis: float32 [16, 1048576], P(None, ('graphs', 'rows', 'cols', 'sub')), parts along dimension 1
- w_image: float32 [16, 1048576], P(None, ('graphs', 'rows', 'cols', 'sub')), parts along dimension 1
- ritz_matrix: float32 [96, 48], P('graphs'), parts along dimension 0
There are 2 independent parts, one for each index of `graphs`. A program takes and returns all parts, laid end to end along the dimension named above; each array names one. Nothing has to cross between parts.
Inputs may be any that keep to these rules, and one draw needn't show every extreme that they name: `current_block`: entries of order one to some hundreds. `previous_block`: entries of order one to some hundreds. Slots d * 48 to (d + 1) * 48 - 1 belong to device d and name its own tile rows d * 16 to (d + 1) * 16 - 1. The first 16 slots of a device name its tile rows in order, with tile_cols equal to tile_rows. Slots past the device's count name tile row d * 16 and carry no weight. `tile_cols`: A slot of device d names a tile column from d * 16 - 8 to (d + 1) * 16 + 7. Slot 16 of a device names a tile of the block before it and slot 17 one of the block after it, where such a block exists. A pair of tile row and tile column may stand in several slots; their tiles add. `tile_count`: in every draw some device has all 48 slots live.
All inputs are finite; a program needn't handle non-finite values.
Results may differ from a plain program's by a relative error of at most 0.000094.
Values sent between devices are 32-bit elements; how exact they have to be, the bound alone decides.
A program may use at most 64 MiB of HBM per device.

v0:
```python
import jax
import jax.numpy as jnp
from jax import lax
from jax.sharding import PartitionSpec as P


def extended(value, sides, width):
    edges = {}
    for axis, dim in sides:
        devices, length = (lax.axis_size(axis), value.shape[dim])
        up = [(i, (i + 1) % devices) for i in range(devices - 1)]
        last = lax.slice_in_dim(value, length - width, length, axis=dim)
        initial = lax.slice_in_dim(value, 0, width, axis=dim)
        edges[dim] = (
            lax.ppermute(last, axis, up),
            lax.ppermute(initial, axis, [(b, a) for a, b in up]),
        )
    done = []
    for _, dim in sides:
        low, high = edges[dim]
        around = [(width, width) if d in done else (0, 0) for d in range(value.ndim)]
        value = jnp.concatenate([jnp.pad(low, around), value, jnp.pad(high, around)], axis=dim)
        done.append(dim)
    return value


def one_axis_at_a_time(value, axes):
    for axis in axes:
        value = lax.psum(value, axis)
    return value


def inner_products(left, right):
    return jnp.dot(left, right.T, precision=lax.Precision.HIGHEST)


def solve_lower(factor, values):
    return lax.linalg.triangular_solve(factor, values, left_side=True, lower=True)


def rayleigh_ritz(gram_b, gram_a):
    factor_b = jnp.linalg.cholesky(gram_b)
    symmetric = 0.5 * (gram_a + gram_a.T)
    halfway = solve_lower(factor_b, symmetric)
    return solve_lower(factor_b, halfway.T)


def operate(vectors, padded, adjacency_tiles, column_position, placing, span_tiles):
    channels, rows_here = vectors.shape
    tile_size = adjacency_tiles.shape[1]
    column_blocks = padded.reshape(channels, span_tiles, tile_size)
    gathered = jnp.take(column_blocks, column_position, axis=1)
    products = jnp.einsum(
        "cta,tab->ctb", gathered, adjacency_tiles, precision=lax.Precision.HIGHEST
    )
    summed = jnp.einsum("ctb,tr->crb", products, placing, precision=lax.Precision.HIGHEST)
    return vectors - summed.reshape(channels, rows_here)


def body(current_block, previous_block, adjacency_tiles, tile_rows, tile_cols, tile_count, locked):
    vectors_k, rows_here = current_block.shape
    tile_size = adjacency_tiles.shape[1]
    row_tiles = rows_here // tile_size
    slot_count = adjacency_tiles.shape[0]
    vertex_total = rows_here * lax.axis_size(("rows", "cols", "sub"))
    position = lax.axis_index(("rows", "cols", "sub"))
    reach_tiles = row_tiles // 2
    span_tiles = row_tiles + 2 * reach_tiles
    column_position = tile_cols - (position * row_tiles - reach_tiles)
    row_slot = tile_rows - position * row_tiles
    live_mask = (jnp.arange(slot_count, dtype=jnp.int32) < tile_count[0]).astype(jnp.float32)
    placing = (row_slot[:, None] == jnp.arange(row_tiles, dtype=jnp.int32)[None, :]).astype(
        jnp.float32
    )
    placing = placing * live_mask[:, None]
    stacked = jnp.concatenate([current_block, previous_block], axis=0)
    padded_pair = extended(stacked, ((("rows", "cols", "sub"), 1),), reach_tiles * tile_size)
    pair_image = operate(
        stacked, padded_pair, adjacency_tiles, column_position, placing, span_tiles
    )
    x_image = pair_image[:vectors_k]
    p_image = pair_image[vectors_k:]
    frozen_rows = jnp.arange(vectors_k, dtype=jnp.int32) < locked[0]
    frozen_diag = jnp.diag(frozen_rows.astype(jnp.float32))
    zero_rows = jnp.zeros((vectors_k,), jnp.float32)
    pad_diag = jnp.diag(jnp.concatenate([zero_rows, frozen_rows.astype(jnp.float32), zero_rows]))
    cross_sum, square_sum = (
        one_axis_at_a_time(jnp.sum(current_block * x_image, axis=1), ("rows", "cols", "sub")),
        one_axis_at_a_time(jnp.sum(current_block * current_block, axis=1), ("rows", "cols", "sub")),
    )
    quotient = cross_sum / (square_sum + 1e-06)
    residual = jnp.where(frozen_rows[:, None], 0.0, x_image - quotient[:, None] * current_block)
    gram_w = (
        one_axis_at_a_time(inner_products(residual, residual), ("rows", "cols", "sub"))
        / vertex_total
        + frozen_diag
    )
    factor = jnp.linalg.cholesky(gram_w)
    w_basis = solve_lower(factor, residual)
    padded = extended(w_basis, ((("rows", "cols", "sub"), 1),), reach_tiles * tile_size)
    w_image = operate(w_basis, padded, adjacency_tiles, column_position, placing, span_tiles)
    search = jnp.concatenate([current_block, w_basis, previous_block], axis=0)
    search_image = jnp.concatenate([x_image, w_image, p_image], axis=0)
    plain_sum, image_sum = (
        one_axis_at_a_time(inner_products(search, search), ("rows", "cols", "sub")),
        one_axis_at_a_time(inner_products(search, search_image), ("rows", "cols", "sub")),
    )
    gram_b = plain_sum / vertex_total + pad_diag
    gram_a = image_sum / vertex_total
    ritz_matrix = rayleigh_ritz(gram_b, gram_a)
    return (w_basis, w_image, ritz_matrix)


def solution(mesh):
    in_specs = (
        P(None, ("graphs", "rows", "cols", "sub")),
        P(None, ("graphs", "rows", "cols", "sub")),
        P(("graphs", "rows", "cols", "sub"), None, None),
        P(("graphs", "rows", "cols", "sub")),
        P(("graphs", "rows", "cols", "sub")),
        P(("graphs", "rows", "cols", "sub")),
        P("graphs"),
    )
    out_specs = (
        P(None, ("graphs", "rows", "cols", "sub")),
        P(None, ("graphs", "rows", "cols", "sub")),
        P("graphs", None),
    )
    return jax.shard_map(body, mesh=mesh, in_specs=in_specs, out_specs=out_specs, check_vma=False)
```

profile of v0, /device:TPU:33, one launch (start us, length us, event | category | flops | bytes accessed | tf_op | source)
XLA Modules:
  0.0 362.2 jit_solution(13121580219357382442)
XLA Ops:
  3.3 4.6 %collective-permute-start = (f32[32,1024]{1,0:T(8,128)}, f32[32,1024]{1,0:T(8,128)}, u32[]{:S(2)}, u32[]{:S(2)}) collective-permute-start(f32[32,1024]{1,0:T(8,128)} %get-tuple-element.22), channel_id=1, source_target_pairs={{0,1},{1,2},{2,3},{3,4},{4,5},{5,6},{6,7},{7,8},{8,9},{9,10},{10,1... | collective-permute-start | bytes 393224 | tf_op jit(solution)/shard_map/ppermute | solution.py:15
  7.9 40.7 %collective-permute-start.1 = (f32[32,1024]{1,0:T(8,128)S(1)}, f32[32,1024]{1,0:T(8,128)}, u32[]{:S(2)}, u32[]{:S(2)}) collective-permute-start(f32[32,1024]{1,0:T(8,128)S(1)} %get-tuple-element.23), channel_id=1, source_target_pairs={{1,0},{2,1},{3,2},{4,3},{5,4},{6,5},{7,6},{8,7},{9,8},{10,9},{11,1... | collective-permute-start | bytes 393224 | tf_op jit(solution)/shard_map/ppermute | solution.py:16
  52.5 1.8 copy_bitcast_fusion
  54.3 2.5 gather_fusion
  56.8 4.0 %fusion.2 = f32[48,32,128]{2,1,0:T(8,128)S(1)} fusion(f32[48,128,128]{2,1,0:T(8,128)S(1)} %copy-done, f32[48,32,128]{2,1,0:T(8,128)} %gather_fusion, pred[48]{0:T(512)(128)(4,1)S(1)} %get-tuple-element.18), kind=kOutput, calls=%fused_computation.5 | convolution fusion | flops 302186496 | bytes 4718640 | tf_op jit(solution)/shard_map/cta,tab->ctb/dot_general | solution.py:53
  63.3 43.8 %all-reduce.1 = (f32[16]{0:T(128)S(1)}, f32[16]{0:T(128)S(1)}) all-reduce(f32[16]{0:T(128)S(1)} %get-tuple-element.5, f32[16]{0:T(128)S(1)} %get-tuple-element.4), channel_id=1, replica_groups=mesh['graphs'=2,'rows'=32,'cols'=4,'sub'=2] {'rows'}, use_global_device_ids=true, to_apply=%region_1.2 | all-reduce | flops 32 | bytes 256 | tf_op jit(solution)/shard_map/psum | solution.py:29
  107.1 8.0 %all-reduce.3 = (f32[16]{0:T(128)S(1)}, f32[16]{0:T(128)S(1)}) all-reduce(f32[16]{0:T(128)S(1)} %get-tuple-element.8, f32[16]{0:T(128)S(1)} %get-tuple-element.9), channel_id=1, replica_groups=mesh['graphs'=2,'rows'=32,'cols'=4,'sub'=2] {'cols'}, use_global_device_ids=true, to_apply=%region_2.3 | all-reduce | flops 32 | bytes 256 | tf_op jit(solution)/shard_map/psum | solution.py:29
  115.2 19.1 %all-reduce.5 = (f32[16]{0:T(128)S(1)}, f32[16]{0:T(128)S(1)}) all-reduce(f32[16]{0:T(128)S(1)} %get-tuple-element.12, f32[16]{0:T(128)S(1)} %get-tuple-element.13), channel_id=1, replica_groups=mesh['graphs'=2,'rows'=32,'cols'=4,'sub'=2] {'sub'}, use_global_device_ids=true, to_apply=%region_3.4 | all-reduce | flops 32 | bytes 256 | tf_op jit(solution)/shard_map/psum | solution.py:29
  134.3 1.3 fusion.53
  135.6 40.0 %psum.111 = f32[16,16]{1,0:T(8,128)S(1)} all-reduce(f32[16,16]{1,0:T(8,128)S(1)} %fusion.53), channel_id=1, replica_groups=mesh['graphs'=2,'rows'=32,'cols'=4,'sub'=2] {'rows'}, use_global_device_ids=true, to_apply=%region_8.9 | all-reduce | flops 256 | bytes 2048 | tf_op jit(solution)/shard_map/psum | solution.py:29
  175.7 6.9 %psum.112 = f32[16,16]{1,0:T(8,128)S(1)} all-reduce(f32[16,16]{1,0:T(8,128)S(1)} %psum.111), channel_id=1, replica_groups=mesh['graphs'=2,'rows'=32,'cols'=4,'sub'=2] {'cols'}, use_global_device_ids=true, to_apply=%region_9.10 | all-reduce | flops 256 | bytes 2048 | tf_op jit(solution)/shard_map/psum | solution.py:29
  182.6 18.4 %psum.113 = f32[16,16]{1,0:T(8,128)S(1)} all-reduce(f32[16,16]{1,0:T(8,128)S(1)} %psum.112), channel_id=1, replica_groups=mesh['graphs'=2,'rows'=32,'cols'=4,'sub'=2] {'sub'}, use_global_device_ids=true, to_apply=%region_10.11 | all-reduce | flops 256 | bytes 2048 | tf_op jit(solution)/shard_map/psum | solution.py:29
  202.5 1.4 cholesky.31
  207.9 2.9 collective-permute-start.2
  210.8 2.0 collective-permute-start.3
  212.8 2.0 fusion.20
  214.8 1.6 collective-permute-done.3
  217.1 2.3 gather_fusion.1
  219.4 3.8 %fusion.14 = f32[48,16,128]{2,1,0:T(8,128)S(1)} fusion(f32[48,128,128]{2,1,0:T(8,128)S(1)} %copy-done, f32[48,16,128]{2,1,0:T(8,128)} %gather_fusion.1, pred[48]{0:T(512)(128)(4,1)S(1)} %get-tuple-element.18), kind=kOutput, calls=%fused_computation.20 | convolution fusion | flops 151093248 | bytes 3932208 | tf_op jit(solution)/shard_map/cta,tab->ctb/dot_general | solution.py:53
  225.5 78.5 %all-reduce = (f32[48,48]{0,1:T(8,128)S(1)}, f32[48,48]{0,1:T(8,128)S(1)}) all-reduce(f32[48,48]{0,1:T(8,128)} %fusion.6, f32[48,48]{0,1:T(8,128)} %fusion.20), channel_id=1, replica_groups=mesh['graphs'=2,'rows'=32,'cols'=4,'sub'=2] {'rows'}, use_global_device_ids=true, to_apply=%region_18.19 | all-reduce | flops 4608 | bytes 36864 | tf_op jit(solution)/shard_map/psum | solution.py:29
  304.0 14.9 %all-reduce.2 = (f32[48,48]{0,1:T(8,128)S(1)}, f32[48,48]{0,1:T(8,128)S(1)}) all-reduce(f32[48,48]{0,1:T(8,128)S(1)} %get-tuple-element.6, f32[48,48]{0,1:T(8,128)S(1)} %get-tuple-element.7), channel_id=1, replica_groups=mesh['graphs'=2,'rows'=32,'cols'=4,'sub'=2] {'cols'}, use_global_device_ids=true, to_apply=%region_19.20 | all-reduce | flops 4608 | bytes 36864 | tf_op jit(solution)/shard_map/psum | solution.py:29
  318.8 32.5 %all-reduce.4 = (f32[48,48]{0,1:T(8,128)S(1)}, f32[48,48]{0,1:T(8,128)S(1)}) all-reduce(f32[48,48]{0,1:T(8,128)S(1)} %get-tuple-element.10, f32[48,48]{0,1:T(8,128)S(1)} %get-tuple-element.11), channel_id=1, replica_groups=mesh['graphs'=2,'rows'=32,'cols'=4,'sub'=2] {'sub'}, use_global_device_ids=true, to_apply=%region_20.21 | all-reduce | flops 4608 | bytes 36864 | tf_op jit(solution)/shard_map/psum | solution.py:29
  351.7 4.4 %cholesky.65 = f32[48,48]{1,0:T(8,128)S(1)} custom-call(f32[48,48]{1,0:T(8,128)S(1)} %fusion.29), custom_call_target="Cholesky" | custom-call | tf_op jit(solution)/shard_map/jit(cholesky)/cholesky | solution.py:42
  357.4 3.7 %custom-call.15 = f32[1,48,48]{1,2,0:T(8,128)S(1)} custom-call(f32[1,48,48]{2,1,0:T(8,128)S(1)} %fusion.23), custom_call_target="InvertDiagBlocksLowerTriangular" | custom-call | tf_op jit(solution)/shard_map/triangular_solve/custom-call.3 | solution.py:38
  (70 shorter events, 18.8 us)
Async XLA Ops:
  0.6 56.2 %copy-start = (f32[48,128,128]{2,1,0:T(8,128)S(1)}, f32[48,128,128]{2,1,0:T(8,128)}, u32[]{:S(2)}) copy-start(f32[48,128,128]{2,1,0:T(8,128)} %param.11) | copy-start | bytes 9437188
  3.3 49.1 %collective-permute-start = (f32[32,1024]{1,0:T(8,128)}, f32[32,1024]{1,0:T(8,128)}, u32[]{:S(2)}, u32[]{:S(2)}) collective-permute-start(f32[32,1024]{1,0:T(8,128)} %get-tuple-element.22), channel_id=1, source_target_pairs={{0,1},{1,2},{2,3},{3,4},{4,5},{5,6},{6,7},{7,8},{8,9},{9,10},{10,1... | collective-permute-start | bytes 393224 | tf_op jit(solution)/shard_map/ppermute | solution.py:15
  7.9 44.6 %collective-permute-start.1 = (f32[32,1024]{1,0:T(8,128)S(1)}, f32[32,1024]{1,0:T(8,128)}, u32[]{:S(2)}, u32[]{:S(2)}) collective-permute-start(f32[32,1024]{1,0:T(8,128)S(1)} %get-tuple-element.23), channel_id=1, source_target_pairs={{1,0},{2,1},{3,2},{4,3},{5,4},{6,5},{7,6},{8,7},{9,8},{10,9},{11,1... | collective-permute-start | bytes 393224 | tf_op jit(solution)/shard_map/ppermute | solution.py:16
  49.3 11.5 %copy-start.7 = (s32[48]{0:T(128)}, s32[48]{0:T(128)S(1)}, u32[]{:S(2)}) copy-start(s32[48]{0:T(128)S(1)} %broadcast_subtract_fusion) | copy-start | bytes 580
  50.0 10.8 %copy-start.9 = (f32[48]{0:T(128)}, f32[48]{0:T(128)S(1)}, u32[]{:S(2)}) copy-start(f32[48]{0:T(128)S(1)} %compare_convert_fusion) | copy-start | bytes 580
  51.1 1.3 copy-start.13
  56.8 5.7 %copy-start.2 = (f32[16,2048]{1,0:T(8,128)S(1)}, f32[16,2048]{1,0:T(8,128)}, u32[]{:S(2)}) copy-start(f32[16,2048]{1,0:T(8,128)} %param.9) | copy-start | bytes 393220
  61.8 0.7 copy-start.1
  134.3 70.4 %copy-start.12 = (f32[16]{0:T(128)}, f32[16]{0:T(128)S(1)}, u32[]{:S(2)}) copy-start(f32[16]{0:T(128)S(1)} %add_divide_fusion) | copy-start | bytes 196
  207.8 15.9 %copy-start.3 = (f32[16,2048]{1,0:T(8,128)}, f32[16,2048]{1,0:T(8,128)S(1)}, u32[]{:S(2)}) copy-start(f32[16,2048]{1,0:T(8,128)S(1)} %fusion.32) | copy-start | bytes 393220
  207.8 15.4 %copy-start.8 = (s32[48]{0:T(128)S(1)}, s32[48]{0:T(128)}, u32[]{:S(2)}) copy-start(s32[48]{0:T(128)} %copy-done.7) | copy-start | bytes 580
  207.8 15.4 %copy-start.10 = (f32[48]{0:T(128)S(1)}, f32[48]{0:T(128)}, u32[]{:S(2)}) copy-start(f32[48]{0:T(128)} %copy-done.9) | copy-start | bytes 580
  207.9 6.9 %collective-permute-start.2 = (f32[16,1024]{1,0:T(8,128)S(1)}, f32[16,1024]{1,0:T(8,128)S(1)}, u32[]{:S(2)}, u32[]{:S(2)}) collective-permute-start(f32[16,1024]{1,0:T(8,128)S(1)} %get-tuple-element.24), channel_id=1, source_target_pairs={{0,1},{1,2},{2,3},{3,4},{4,5},{5,6},{6,7},{7,8},{8,9},{9,10},{10,1... | collective-permute-start | bytes 196616 | tf_op jit(solution)/shard_map/ppermute | solution.py:15
  210.8 5.6 %collective-permute-start.3 = (f32[16,1024]{1,0:T(8,128)S(1)}, f32[16,1024]{1,0:T(8,128)S(1)}, u32[]{:S(2)}, u32[]{:S(2)}) collective-permute-start(f32[16,1024]{1,0:T(8,128)S(1)} %get-tuple-element.25), channel_id=1, source_target_pairs={{1,0},{2,1},{3,2},{4,3},{5,4},{6,5},{7,6},{8,7},{9,8},{10,9},{11,1... | collective-permute-start | bytes 196616 | tf_op jit(solution)/shard_map/ppermute | solution.py:16
  219.4 5.0 %copy-start.4 = (f32[16,2048]{1,0:T(8,128)S(1)}, f32[16,2048]{1,0:T(8,128)}, u32[]{:S(2)}) copy-start(f32[16,2048]{1,0:T(8,128)} %get-tuple-element.21) | copy-start | bytes 393220
  219.4 5.0 %copy-start.6 = (f32[16,2048]{1,0:T(8,128)S(1)}, f32[16,2048]{1,0:T(8,128)}, u32[]{:S(2)}) copy-start(f32[16,2048]{1,0:T(8,128)} %param.10) | copy-start | bytes 393220
  219.4 132.0 %copy-start.11 = (f32[48]{0:T(128)S(1)}, f32[48]{0:T(128)}, u32[]{:S(2)}) copy-start(f32[48]{0:T(128)} %pad_maximum_fusion.3) | copy-start | bytes 580
  223.7 0.7 copy-start.5
where the time goes:
time: 363 us; the launch traced here: 362 us
  blocking collectives  262 us (72%)
  starting transfers between devices  50.2 us (14%)
  other arithmetic  21 us (6%)
  matrix products  15.9 us (4%)
  local copies, waits for them, and re-layouts  9.13 us (3%)
    psum x9, blocking collectives, one_axis_at_a_time(): value = lax.psum(value, axis)  262 us
    ppermute x2, starting transfers between devices, extended(): lax.ppermute(initial, axis, [(b, a) for a, b in up])  42.7 us
    dot_general x2, matrix products, operate(): jnp.einsum('cta,tab->ctb', gathered, adjacency_tiles, precision=lax.Preci...  7.81 us
    ppermute x2, starting transfers between devices, extended(): lax.ppermute(last, axis, up)  7.51 us
  transfers between devices with their start and end apart: 4, of which 1 were waited for; matrix products, arithmetic and copies ran while one was open for 1% of the time, Pallas kernels for 0%

commit v1 on v0

v1 whole, which is shorter than its diff:
```python
import functools

import jax
import jax.numpy as jnp
from jax import lax
from jax.experimental import pallas as pl
from jax.experimental.pallas import tpu as pltpu
from jax.sharding import PartitionSpec as P

MESH = pl.DeviceIdType.MESH
F32 = jnp.float32
BF16 = jnp.bfloat16
VMEM = pltpu.VMEM
VERTEX_AXES = ("rows", "cols", "sub")
CHUNKS = 4
GROUP = 8
PACKED = 32


def halves(value):
    high = value.astype(BF16)
    return high, (value - high.astype(F32)).astype(BF16)


def fill_tiles(split, first, value):
    width = split.shape[2]
    for i in range(value.shape[1] // width):
        split[first + i] = jnp.concatenate(halves(value[:, i * width : (i + 1) * width]), axis=0)


def tile_copies(tiles_ref, tiles, sems):
    each = tiles.shape[0] // CHUNKS
    return [
        pltpu.make_async_copy(
            tiles_ref.at[pl.ds(i * each, each)], tiles.at[pl.ds(i * each, each)], sems.at[i]
        )
        for i in range(CHUNKS)
    ]


def slot_product(left, tile):
    channels = left.shape[0] // 2
    high, low = halves(tile)
    both = jnp.concatenate([high, low], axis=1)
    out = jnp.dot(left, both, preferred_element_type=F32)
    width = tile.shape[1]
    top, bottom = out[:channels], out[channels:]
    return (top[:, :width] + (top[:, width:] + bottom[:, :width])) + bottom[:, width:]


def products(split, tiles, prods, first, last, column):
    def step(block, carry):
        for lane in range(GROUP):
            slot = block * GROUP + lane
            prods[slot] = slot_product(split[column(slot)], tiles[slot])
        return carry

    lax.fori_loop(first // GROUP, last // GROUP, step, 0)


def summed_rows(prods, rows_s, count_s, base, row_tiles, store):
    slots = prods.shape[0]
    count = count_s[0]
    for block in range(row_tiles // 4):
        mine = [block * 4 + i for i in range(4)]

        def step(slot, sums):
            value = prods[slot]
            row = rows_s[slot] - base
            live = jnp.clip(count - slot, 0, 1)
            return tuple(
                s + (live * (1 - jnp.minimum(jnp.abs(row - i), 1))).astype(F32) * value
                for i, s in zip(mine, sums)
            )

        sums = lax.fori_loop(
            row_tiles, slots, step, tuple(prods[i] for i in mine), unroll=8
        )
        for i, s in zip(mine, sums):
            store(i, s)


def place(sizes):
    rows, cols, sub = (lax.axis_index(a) for a in VERTEX_AXES)
    return (rows * sizes[1] + cols) * sizes[2] + sub


def device_at(position, sizes):
    return {
        "rows": position // (sizes[1] * sizes[2]),
        "cols": (position // sizes[2]) % sizes[1],
        "sub": position % sizes[2],
    }


def first_kernel(
    sizes, x, p, tiles_ref, rows_s, cols_s, count_s, yext, q,
    tiles, wide, split, ywide, prods, tile_sems, send, recv,
):
    channels, here = x.shape
    width = tiles.shape[1]
    row_tiles = here // width
    reach = here // 2
    total = sizes[0] * sizes[1] * sizes[2]
    me = place(sizes)
    base = me * row_tiles
    loads = tile_copies(tiles_ref, tiles, tile_sems)
    for load in loads:
        load.start()
    has_low, has_high = me > 0, me < total - 1
    low, high = device_at(me - 1, sizes), device_at(me + 1, sizes)
    barrier = pltpu.get_barrier_semaphore()

    @pl.when(has_low)
    def _():
        pl.semaphore_signal(barrier, inc=1, device_id=low, device_id_type=MESH)

    @pl.when(has_high)
    def _():
        pl.semaphore_signal(barrier, inc=1, device_id=high, device_id_type=MESH)

    pl.semaphore_wait(barrier, has_low.astype(jnp.int32) + has_high.astype(jnp.int32))

    def remote(source, target, n, device):
        return pltpu.make_async_remote_copy(
            src_ref=source, dst_ref=target, send_sem=send.at[n], recv_sem=recv.at[n],
            device_id=device, device_id_type=MESH,
        )

    own = pl.ds(reach, here)
    low_side, high_side = pl.ds(0, reach), pl.ds(reach + here, reach)
    to_low = [
        remote(v.at[:, pl.ds(0, reach)], wide.at[pl.ds(i * channels, channels), high_side], i, low)
        for i, v in enumerate((x, p))
    ]
    to_high = [
        remote(
            v.at[:, pl.ds(here - reach, reach)],
            wide.at[pl.ds(i * channels, channels), low_side], 2 + i, high,
        )
        for i, v in enumerate((x, p))
    ]
    y_low = remote(ywide.at[:, pl.ds(reach, reach)], ywide.at[:, high_side], 4, low)
    y_high = remote(ywide.at[:, pl.ds(here, reach)], ywide.at[:, low_side], 5, high)

    @pl.when(has_low)
    def _():
        for copy in to_low:
            copy.start()

    @pl.when(has_high)
    def _():
        for copy in to_high:
            copy.start()

    def fill(first, value):
        fill_tiles(split, first, value)

    reach_tiles = reach // width
    fill(reach_tiles, jnp.concatenate([x[...], p[...]], axis=0))
    loads[0].wait()
    loads[1].wait()
    products(split, tiles, prods, 0, row_tiles, lambda slot: slot + reach_tiles)

    @pl.when(has_low)
    def _():
        for copy in to_low:
            copy.wait_send()
        for copy in to_high:
            copy.wait_recv()

    @pl.when(has_high)
    def _():
        for copy in to_high:
            copy.wait_send()
        for copy in to_low:
            copy.wait_recv()

    @pl.when(jnp.logical_not(has_low))
    def _():
        wide[:, low_side] = jnp.zeros((2 * channels, reach), F32)
        ywide[:, low_side] = jnp.zeros((channels, reach), F32)

    @pl.when(jnp.logical_not(has_high))
    def _():
        wide[:, high_side] = jnp.zeros((2 * channels, reach), F32)
        ywide[:, high_side] = jnp.zeros((channels, reach), F32)

    fill(0, wide[:, low_side])
    fill(reach_tiles + row_tiles, wide[:, high_side])
    for load in loads[2:]:
        load.wait()
    products(
        split, tiles, prods, row_tiles, tiles.shape[0],
        lambda slot: jnp.clip(cols_s[slot] - (base - reach_tiles), 0, split.shape[0] - 1),
    )

    def store(i, value):
        ywide[:, pl.ds(reach + i * width, width)] = value[:channels]
        q[:, pl.ds(i * width, width)] = value[channels:]

    summed_rows(prods, rows_s, count_s, base, row_tiles, store)

    @pl.when(has_low)
    def _():
        y_low.start()

    @pl.when(has_high)
    def _():
        y_high.start()

    yext[:, own] = ywide[:, own]

    @pl.when(has_low)
    def _():
        y_low.wait_send()
        y_high.wait_recv()

    @pl.when(has_high)
    def _():
        y_high.wait_send()
        y_low.wait_recv()

    yext[:, low_side] = ywide[:, low_side]
    yext[:, high_side] = ywide[:, high_side]


def second_kernel(
    sizes, x, p, q, yext, tiles_ref, rows_s, cols_s, count_s, total_ref, z,
    tiles, split, prods, parts, arrived, along, gathered, tile_sems,
    send_a, recv_a, send_b, recv_b, send_c, recv_c,
):
    channels, here = x.shape
    width = tiles.shape[1]
    row_tiles = here // width
    reach = here // 2
    reach_tiles = reach // width
    depth, cols, sub = sizes
    members = cols * sub
    me = place(sizes)
    base = me * row_tiles
    layer = lax.axis_index("rows")
    member = lax.axis_index("cols") * sub + lax.axis_index("sub")
    barrier = pltpu.get_barrier_semaphore()
    loads = tile_copies(tiles_ref, tiles, tile_sems)
    for load in loads:
        load.start()

    def layer_at(k):
        half = (k + 1) // 2
        offset = jnp.where(k % 2 == 1, half, -half)
        return (layer + depth // 2 + depth + offset) % depth

    def member_at(k):
        other = (member + k + 1) % members
        return other, {"cols": other // sub, "sub": other % sub}

    def greet_layer(k, carry):
        pl.semaphore_signal(barrier, inc=1, device_id={"rows": layer_at(k)}, device_id_type=MESH)
        return carry

    def greet_member(k, carry):
        pl.semaphore_signal(barrier, inc=1, device_id=member_at(k)[1], device_id_type=MESH)
        return carry

    lax.fori_loop(0, depth - 1, greet_layer, 0)
    lax.fori_loop(0, members - 1, greet_member, 0)

    fill_tiles(split, 0, yext[...])
    for load in loads:
        load.wait()
    products(split, tiles, prods, 0, row_tiles, lambda slot: slot + reach_tiles)
    products(
        split, tiles, prods, row_tiles, tiles.shape[0],
        lambda slot: jnp.clip(cols_s[slot] - (base - reach_tiles), 0, split.shape[0] - 1),
    )

    def store(i, value):
        z[:, pl.ds(i * width, width)] = value

    summed_rows(prods, rows_s, count_s, base, row_tiles, store)

    xs, ps = x[...], p[...]
    ys = yext[:, pl.ds(reach, here)]
    left = jnp.concatenate([xs, ys, ps], axis=0)
    right = jnp.concatenate([xs, ys, z[...], ps, q[...]], axis=0)
    right = jnp.concatenate([right, jnp.zeros((128 - 5 * channels, here), F32)], axis=0)
    gram = lax.dot_general(
        left, right, (((1,), (1,)), ((), ())), precision=lax.Precision.HIGHEST,
        preferred_element_type=F32,
    )
    lane = lax.broadcasted_iota(jnp.int32, (channels, 128), 1)
    turned = pltpu.roll(gram[2 * channels :], 3 * channels, 1)
    packed = jnp.concatenate(
        [jnp.where(lane < 5 * channels, gram[:channels], turned), gram[channels : 2 * channels]],
        axis=0,
    )
    rows_each = PACKED // members
    for i in range(members):
        parts[i] = packed[i * rows_each : (i + 1) * rows_each]

    pl.semaphore_wait(barrier, depth - 1 + members - 1)

    def spread(k):
        other, device = member_at(k)
        return pltpu.make_async_remote_copy(
            src_ref=parts.at[other], dst_ref=arrived.at[member], send_sem=send_a.at[other],
            recv_sem=recv_a.at[member], device_id=device, device_id_type=MESH,
        )

    def spread_in(k):
        other, device = member_at(k)
        return pltpu.make_async_remote_copy(
            src_ref=parts.at[other], dst_ref=arrived.at[other], send_sem=send_a.at[other],
            recv_sem=recv_a.at[other], device_id=device, device_id_type=MESH,
        )

    def over(k):
        other = layer_at(k)
        return pltpu.make_async_remote_copy(
            src_ref=along.at[layer], dst_ref=along.at[layer], send_sem=send_b.at[other],
            recv_sem=recv_b.at[layer], device_id={"rows": other}, device_id_type=MESH,
        )

    def over_in(k):
        other = layer_at(k)
        return pltpu.make_async_remote_copy(
            src_ref=along.at[layer], dst_ref=along.at[other], send_sem=send_b.at[other],
            recv_sem=recv_b.at[other], device_id={"rows": other}, device_id_type=MESH,
        )

    def share(k):
        other, device = member_at(k)
        return pltpu.make_async_remote_copy(
            src_ref=gathered.at[member], dst_ref=gathered.at[member], send_sem=send_c.at[other],
            recv_sem=recv_c.at[member], device_id=device, device_id_type=MESH,
        )

    def share_in(k):
        other, device = member_at(k)
        return pltpu.make_async_remote_copy(
            src_ref=gathered.at[member], dst_ref=gathered.at[other], send_sem=send_c.at[other],
            recv_sem=recv_c.at[other], device_id=device, device_id_type=MESH,
        )

    def each(n, act):
        def step(k, carry):
            act(k)
            return carry

        lax.fori_loop(0, n, step, 0)

    each(members - 1, lambda k: spread(k).start())
    arrived[member] = parts[member]
    each(members - 1, lambda k: spread_in(k).wait_recv())
    along[layer] = jnp.sum(arrived[...], axis=0)
    each(depth - 1, lambda k: over(k).start())
    each(depth - 1, lambda k: over_in(k).wait_recv())
    gathered[member] = jnp.sum(along[...], axis=0)
    each(members - 1, lambda k: share(k).start())
    each(members - 1, lambda k: share_in(k).wait_recv())
    total_ref[...] = gathered[...]
    each(members - 1, lambda k: spread(k).wait_send())
    each(depth - 1, lambda k: over(k).wait_send())
    each(members - 1, lambda k: share(k).wait_send())


def eliminated(matrix):
    n = matrix.shape[0]
    row = lax.broadcasted_iota(jnp.int32, (n, 1), 0)
    pivots = []
    for k in range(n):
        top = matrix[k : k + 1]
        pivot = top[:, k : k + 1]
        pivots.append(pivot)
        if k < n - 1:
            scaled = top * (1.0 / pivot)
            matrix = matrix - jnp.where(row > k, matrix[:, k : k + 1], 0.0) * scaled
    return matrix * lax.rsqrt(jnp.concatenate(pivots, axis=0))


def precise(left, right, turned=False):
    return lax.dot_general(
        left, right, (((1,), (1 if turned else 0,)), ((), ())),
        precision=lax.Precision.HIGHEST, preferred_element_type=F32,
    )


def third_kernel(vertex_total, total_ref, x, yext, z, locked_s, w, w_image, ritz):
    channels, here = x.shape
    reach = here // 2
    packed = jnp.concatenate([total_ref[i] for i in range(total_ref.shape[0])], axis=0)
    first, second = packed[:channels], packed[channels:]

    def part(v, i):
        return v[:, i * channels : (i + 1) * channels]

    xx, xy, xz, xp, xq = (part(first, i) for i in range(5))
    pz, pp, pq = (part(first, i) for i in range(5, 8))
    yp = part(second, 3)
    shape = (channels, channels)
    row = lax.broadcasted_iota(jnp.int32, shape, 0)
    column = lax.broadcasted_iota(jnp.int32, shape, 1)
    eye = jnp.where(row == column, 1.0, 0.0).astype(F32)
    locked = locked_s[0]
    top = eye * (xy + 1e-06)
    below = eye * (xx + 1e-06)
    c_down = jnp.sum(top, axis=1, keepdims=True) / jnp.sum(below, axis=1, keepdims=True)
    c_along = jnp.sum(top, axis=0, keepdims=True) / jnp.sum(below, axis=0, keepdims=True)
    free_down = (lax.broadcasted_iota(jnp.int32, (channels, 1), 0) >= locked).astype(F32)
    free_along = (lax.broadcasted_iota(jnp.int32, (1, channels), 1) >= locked).astype(F32)
    scale = 1.0 / vertex_total
    frozen = eye * (1.0 - free_down)
    rd = free_down * (c_down * first - second)
    rx, ry = part(rd, 0), part(rd, 1)
    gram_w = free_along * (rx * c_along - ry) * scale + frozen
    inverse = eliminated(jnp.concatenate([gram_w, eye], axis=1))[:, channels:]

    xs, ys, zs = x[...], yext[:, pl.ds(reach, here)], z[...]
    r = free_down * (c_down * xs - ys)
    nr = free_down * (c_down * ys - zs)
    w[...] = precise(inverse, r)
    w_image[...] = precise(inverse, r - nr)

    wd = precise(inverse, rd)
    wx, wy, wz, wp, wq = (part(wd, i) for i in range(5))
    px, py = xp.T, yp.T

    def against_r(vx, vy):
        return free_along * (vx * c_along - vy)

    def against_image(vx, vy, vz):
        return free_along * (c_along * (vx - vy) - vy + vz)

    stacked = jnp.concatenate(
        [against_r(wx, wy), against_image(xx, xy, xz), against_image(wx, wy, wz),
         against_image(px, py, pz)], axis=0,
    )
    stacked = precise(stacked, inverse, turned=True)
    ww, xaw, waw, paw = (stacked[i * channels : (i + 1) * channels] for i in range(4))
    gram_b = jnp.concatenate(
        [
            jnp.concatenate([xx, wx.T, xp], axis=1) * scale,
            jnp.concatenate([wx * scale, ww * scale + frozen, wp * scale], axis=1),
            jnp.concatenate([px, wp.T, pp], axis=1) * scale,
        ], axis=0,
    )
    gram_a = jnp.concatenate(
        [
            jnp.concatenate([xx - xy, xaw, xp - xq], axis=1),
            jnp.concatenate([wx - wy, waw, wp - wq], axis=1),
            jnp.concatenate([px - py, paw, pp - pq], axis=1),
        ], axis=0,
    ) * scale
    n = 3 * channels
    big = (
        lax.broadcasted_iota(jnp.int32, (n, n), 0) == lax.broadcasted_iota(jnp.int32, (n, n), 1)
    ).astype(F32)
    lower = eliminated(jnp.concatenate([gram_b, big], axis=1))[:, n:]
    symmetric = 0.5 * (gram_a + gram_a.T)
    ritz[...] = precise(precise(lower, symmetric), lower, turned=True)


def body(sizes, current_block, previous_block, adjacency_tiles, tile_rows, tile_cols, tile_count, locked):
    channels, here = current_block.shape
    slots, width, _ = adjacency_tiles.shape
    depth, cols, sub = sizes
    members = cols * sub
    rows_each = PACKED // members
    vmem = pl.BlockSpec(memory_space=pltpu.VMEM)
    smem = pl.BlockSpec(memory_space=pltpu.SMEM)
    anywhere = pl.BlockSpec(memory_space=pl.ANY)
    dma = pltpu.SemaphoreType.DMA

    def like(*shape):
        return jax.ShapeDtypeStruct(shape, F32)

    yext, q = pl.pallas_call(
        functools.partial(first_kernel, sizes),
        name="first",
        out_shape=(like(channels, 2 * here), like(channels, here)),
        in_specs=[vmem, vmem, anywhere, smem, smem, smem],
        out_specs=(vmem, vmem),
        scratch_shapes=[
            VMEM((slots, width, width), F32),
            VMEM((2 * channels, 2 * here), F32),
            VMEM((2 * here // width, 4 * channels, width), BF16),
            VMEM((channels, 2 * here), F32),
            VMEM((slots, 2 * channels, width), F32),
            dma((CHUNKS,)), dma((6,)), dma((6,)),
        ],
        compiler_params=pltpu.CompilerParams(collective_id=0, has_side_effects=True),
    )(current_block, previous_block, adjacency_tiles, tile_rows, tile_cols, tile_count)
    total, z = pl.pallas_call(
        functools.partial(second_kernel, sizes),
        name="second",
        out_shape=(like(members, rows_each, 128), like(channels, here)),
        in_specs=[vmem, vmem, vmem, vmem, anywhere, smem, smem, smem],
        out_specs=(vmem, vmem),
        scratch_shapes=[
            VMEM((slots, width, width), F32),
            VMEM((2 * here // width, 2 * channels, width), BF16),
            VMEM((slots, channels, width), F32),
            VMEM((members, rows_each, 128), F32),
            VMEM((members, rows_each, 128), F32),
            VMEM((depth, rows_each, 128), F32),
            VMEM((members, rows_each, 128), F32),
            dma((CHUNKS,)),
            dma((members,)), dma((members,)),
            dma((depth,)), dma((depth,)),
            dma((members,)), dma((members,)),
        ],
        compiler_params=pltpu.CompilerParams(collective_id=1, has_side_effects=True),
    )(current_block, previous_block, q, yext, adjacency_tiles, tile_rows, tile_cols, tile_count)
    vertex_total = here * depth * members
    return pl.pallas_call(
        functools.partial(third_kernel, float(vertex_total)),
        name="third",
        out_shape=(like(channels, here), like(channels, here), like(3 * channels, 3 * channels)),
        in_specs=[vmem, vmem, vmem, vmem, smem],
        out_specs=(vmem, vmem, vmem),
    )(total, current_block, yext, z, locked)


def solution(mesh):
    sizes = tuple(mesh.shape[a] for a in VERTEX_AXES)
    everywhere = ("graphs", "rows", "cols", "sub")
    in_specs = (
        P(None, everywhere),
        P(None, everywhere),
        P(everywhere, None, None),
        P(everywhere),
        P(everywhere),
        P(everywhere),
        P("graphs"),
    )
    out_specs = (P(None, everywhere), P(None, everywhere), P("graphs", None))
    return jax.shard_map(
        functools.partial(body, sizes), mesh=mesh, in_specs=in_specs, out_specs=out_specs,
        check_vma=False,
    )
```

time: 363 us -> 103 us (0.28)
  blocking collectives: 262 us -> 0 us
  Pallas kernels: 0 us -> 101 us
  starting transfers between devices: 50.2 us -> 0 us
  other arithmetic: 21 us -> 0 us
  matrix products: 15.9 us -> 0 us
  local copies, waits for them, and re-layouts: 9.13 us -> 0 us
    psum x9 -> x0, blocking collectives: 262 us -> none  [one_axis_at_a_time(): value = lax.psum(value, axis)]
    pallas_call x0 -> x3, Pallas kernels: none -> 101 us  [the longest x1 53.2 us: body(): pl.pallas_call(functools.partial(first_kernel, sizes), name='first', out_...]
    ppermute x4 -> x0, starting transfers between devices: 50.2 us -> none  [the longest x2 42.7 us: extended(): lax.ppermute(initial, axis, [(b, a) for a, b in up])]
    dot_general x7 -> x0, matrix products: 13.6 us -> none  [the longest x2 7.81 us: operate(): jnp.einsum('cta,tab->ctb', gathered, adjacency_tiles, precision=lax.Preci...]
    another operation x10 -> x0, other arithmetic: 13.4 us -> none  [the longest x4 6.2 us: solve_lower(): lax.linalg.triangular_solve(factor, values, left_side=True, lower=True)]
    gather x2 -> x0, local copies, waits for them, and re-layouts: 4.78 us -> none  [operate(): gathered = jnp.take(column_blocks, column_position, axis=1)]
  transfers between devices with their start and end apart: 4 -> 0, of which waited for: 1 -> 0; matrix products, arithmetic and copies ran while one was open for 1% -> 0% of each run, Pallas kernels for 0% -> 0%
where the time goes in v1:
time: 103 us
  Pallas kernels  101 us (98%)
  between operations  1.94 us (2%)
    pallas_call x1, Pallas kernels, body(): pl.pallas_call(functools.partial(first_kernel, sizes), name='first', out_...  53.2 us
    pallas_call x1, Pallas kernels, body(): pl.pallas_call(functools.partial(second_kernel, sizes), name='second', ou...  39.7 us
    pallas_call x1, Pallas kernels, body(): pl.pallas_call(functools.partial(third_kernel, float(vertex_total)), name...  8.42 us

profile of v1, /device:TPU:33, one launch (start us, length us, event | category | flops | bytes accessed | tf_op | source)
XLA Modules:
  0.0 103.2 jit_solution(13952390978539777137)
XLA Ops:
  1.9 53.2 %first.1 = (f32[16,4096]{1,0:T(8,128)}, f32[16,2048]{1,0:T(8,128)}) custom-call(f32[16,2048]{1,0:T(8,128)} %x.5, f32[16,2048]{1,0:T(8,128)} %p.3, f32[48,128,128]{2,1,0:T(8,128)} %tiles_ref.3, s32[48]{0:T(128)} %rows_s.3, s32[48]{0:T(128)} %cols_s.3, s32[1]{0:T(128)S(6)} %copy.10.count_s), custom_call_target="tpu_custom_call" | custom-call | tf_op jit(solution)/shard_map/first/pallas_call | solution.py:478
  55.1 39.7 %second.1 = (f32[8,4,128]{2,1,0:T(4,128)}, f32[16,2048]{1,0:T(8,128)}) custom-call(f32[16,2048]{1,0:T(8,128)} %x.5, f32[16,2048]{1,0:T(8,128)} %p.3, f32[16,2048]{1,0:T(8,128)} %get-tuple-element.7.q, f32[16,4096]{1,0:T(8,128)} %get-tuple-element.8.yext, f32[48,128,128]{2,1,0:T(8,128)} %tiles_ref.3, s32[48]{0:T(128)} %rows_s.3, s32[48]{0:T(128)} %cols_s.3, ...), custom_call_target="tpu_custom_call" | custom-call | tf_op jit(solution)/shard_map/second/pallas_call | solution.py:494
  94.8 8.4 %third.1 = (f32[16,2048]{1,0:T(8,128)}, f32[16,2048]{1,0:T(8,128)}, f32[48,48]{1,0:T(8,128)}) custom-call(f32[8,4,128]{2,1,0:T(4,128)} %get-tuple-element.9.total_ref, f32[16,2048]{1,0:T(8,128)} %x.5, f32[16,4096]{1,0:T(8,128)} %get-tuple-element.8.yext, f32[16,2048]{1,0:T(8,128)} %get-tuple-element.10.z, s32[1]{0:T(128)S(6)} %copy.11.locked_s), custom_call_target="tpu_custom_call" | custom-call | tf_op jit(solution)/shard_map/third/pallas_call | solution.py:516

commit v2 on v0

v2 whole, which is shorter than its diff:
```python
import functools

import jax
import jax.numpy as jnp
from jax import lax
from jax.experimental import pallas as pl
from jax.experimental.pallas import tpu as pltpu
from jax.sharding import PartitionSpec as P

MESH = pl.DeviceIdType.MESH
F32 = jnp.float32
BF16 = jnp.bfloat16
VMEM = pltpu.VMEM
VERTEX_AXES = ("rows", "cols", "sub")
CHUNKS = 4
GROUP = 8
PACKED = 24


def halves(value):
    high = value.astype(BF16)
    return high, (value - high.astype(F32)).astype(BF16)


def tile_copies(tiles_ref, tiles, sems):
    each = tiles.shape[0] // CHUNKS
    return [
        pltpu.make_async_copy(
            tiles_ref.at[pl.ds(i * each, each)], tiles.at[pl.ds(i * each, each)], sems.at[i]
        )
        for i in range(CHUNKS)
    ]


def fill_tiles(split, first, value):
    width = split.shape[2]
    for i in range(value.shape[1] // width):
        split[first + i] = jnp.concatenate(halves(value[:, i * width : (i + 1) * width]), axis=0)


def split_tiles(tiles, pairs, first, last):
    def step(block, carry):
        for lane in range(GROUP // 2):
            slot = block * (GROUP // 2) + lane
            pairs[slot] = jnp.concatenate(halves(tiles[slot]), axis=1)
        return carry

    lax.fori_loop(first // (GROUP // 2), last // (GROUP // 2), step, 0)


def products(split, pairs, prods, first, last, column):
    width = pairs.shape[1]
    channels = split.shape[1] // 2

    def step(block, carry):
        for lane in range(GROUP):
            slot = block * GROUP + lane
            out = jnp.dot(split[column(slot)], pairs[slot], preferred_element_type=F32)
            top, bottom = out[:channels], out[channels:]
            prods[slot] = (
                top[:, :width] + (top[:, width:] + bottom[:, :width])
            ) + bottom[:, width:]
        return carry

    lax.fori_loop(first // GROUP, last // GROUP, step, 0)


def summed_rows(prods, codes, row_tiles, store):
    slots, channels, width = prods.shape
    size = row_tiles // 2
    for block in range(2):
        mine = [block * size + i for i in range(size)]

        def step(slot, sums):
            value = prods[slot]
            row = jnp.full((channels, width), codes[slot], jnp.int32)
            return tuple(s + jnp.where(row == i, value, 0.0) for i, s in zip(mine, sums))

        sums = lax.fori_loop(
            row_tiles, slots, step, tuple(prods[i] for i in mine), unroll=4
        )
        for i, s in zip(mine, sums):
            store(i, s)


def place(sizes):
    rows, cols, sub = (lax.axis_index(a) for a in VERTEX_AXES)
    return (rows * sizes[1] + cols) * sizes[2] + sub


def device_at(position, sizes):
    return {
        "rows": position // (sizes[1] * sizes[2]),
        "cols": (position // sizes[2]) % sizes[1],
        "sub": position % sizes[2],
    }


def main_kernel(
    sizes, x_any, p_any, tiles_any, rows_any, cols_any, count_any, total_ref, y_any, z_any,
    xw, pw, yw, sx, sp, sy, tiles, pairs, prods, q, z, parts, arrived, along, gathered,
    rows_s, cols_s, count_s, codes, load_sems, tile_sems, halo_send, halo_recv,
    send_a, recv_a, send_b, recv_b, send_c, recv_c, out_sems, middle, far,
):
    channels, here = q.shape
    slots, width, _ = tiles.shape
    row_tiles = here // width
    reach = here // 2
    reach_tiles = reach // width
    depth, cols, sub = sizes
    members = cols * sub
    total = depth * members
    me = place(sizes)
    base = me * row_tiles
    layer = lax.axis_index("rows")
    member = lax.axis_index("cols") * sub + lax.axis_index("sub")
    near = depth // 8
    own = pl.ds(reach, here)
    low_side, high_side = pl.ds(0, reach), pl.ds(reach + here, reach)

    def layer_by(offset):
        other = layer + offset
        other = jnp.where(other >= depth, other - depth, other)
        return jnp.where(other < 0, other + depth, other)

    def layer_at(k):
        half = (k + 1) // 2
        return layer_by(depth // 2 + jnp.where(k % 2 == 1, half, -half))

    def member_by(offset):
        other = member + offset
        other = jnp.where(other >= members, other - members, other)
        return other, {"cols": other // sub, "sub": other % sub}

    def each(n, act):
        def step(k, carry):
            act(k)
            return carry

        lax.fori_loop(0, n, step, 0)

    barrier = pltpu.get_barrier_semaphore()

    def greet(semaphore, device):
        pl.semaphore_signal(semaphore, inc=1, device_id=device, device_id_type=MESH)

    has_low, has_high = me > 0, me < total - 1
    low, high = device_at(me - 1, sizes), device_at(me + 1, sizes)

    @pl.when(has_low)
    def _():
        greet(barrier, low)

    @pl.when(has_high)
    def _():
        greet(barrier, high)

    load_x = pltpu.make_async_copy(x_any, xw.at[:, own], load_sems.at[0])
    load_p = pltpu.make_async_copy(p_any, pw.at[:, own], load_sems.at[1])
    small = [
        pltpu.make_async_copy(source, target, load_sems.at[2 + i])
        for i, (source, target) in enumerate(
            ((rows_any, rows_s), (cols_any, cols_s), (count_any, count_s))
        )
    ]
    loads = tile_copies(tiles_any, tiles, tile_sems)
    for load in [load_x, load_p, *small, *loads]:
        load.start()
    for offset in range(1, members):
        greet(barrier, member_by(offset)[1])
    for offset in range(1, near + 1):
        greet(barrier, {"rows": layer_by(offset)})
        greet(barrier, {"rows": layer_by(-offset)})
    pl.semaphore_wait(
        barrier,
        has_low.astype(jnp.int32) + has_high.astype(jnp.int32) + (members - 1 + 2 * near),
    )

    def halo(wide, n):
        def remote(source, target, k, device):
            return pltpu.make_async_remote_copy(
                src_ref=wide.at[:, source], dst_ref=wide.at[:, target],
                send_sem=halo_send.at[k], recv_sem=halo_recv.at[k],
                device_id=device, device_id_type=MESH,
            )

        down = remote(pl.ds(reach, reach), high_side, 2 * n, low)
        up = remote(pl.ds(here, reach), low_side, 2 * n + 1, high)

        def start():
            @pl.when(has_low)
            def _():
                down.start()

            @pl.when(has_high)
            def _():
                up.start()

        def arrive():
            @pl.when(has_low)
            def _():
                up.wait_recv()

            @pl.when(has_high)
            def _():
                down.wait_recv()

        def finish():
            @pl.when(has_low)
            def _():
                down.wait_send()

            @pl.when(has_high)
            def _():
                up.wait_send()

        return start, arrive, finish

    x_start, x_arrive, x_finish = halo(xw, 0)
    p_start, p_arrive, p_finish = halo(pw, 1)
    y_start, y_arrive, y_finish = halo(yw, 2)

    load_x.wait()
    x_start()
    load_p.wait()
    p_start()
    greet(middle, {"rows": layer_by(near)})
    greet(middle, {"rows": layer_by(-near)})

    @pl.when(jnp.logical_not(has_low))
    def _():
        for wide in (xw, pw, yw):
            wide[:, low_side] = jnp.zeros((channels, reach), F32)

    @pl.when(jnp.logical_not(has_high))
    def _():
        for wide in (xw, pw, yw):
            wide[:, high_side] = jnp.zeros((channels, reach), F32)

    for load in small:
        load.wait()
    count = count_s[0]

    def code(slot):
        codes[slot] = jnp.where(slot < count, rows_s[slot] - base, -1)

    each(slots, code)

    def column(slot):
        return jnp.clip(cols_s[slot] - (base - reach_tiles), 0, 2 * row_tiles - 1)

    def inner(split):
        products(split, pairs, prods, 0, row_tiles, lambda slot: slot + reach_tiles)

    def outer(split):
        products(split, pairs, prods, row_tiles, slots, column)

    def fill_own(split, wide):
        fill_tiles(split, reach_tiles, wide[:, own])

    def fill_sides(split, wide):
        fill_tiles(split, 0, wide[:, low_side])
        fill_tiles(split, reach_tiles + row_tiles, wide[:, high_side])

    fill_own(sx, xw)
    for i, load in enumerate(loads):
        load.wait()
        split_tiles(tiles, pairs, i * slots // CHUNKS, (i + 1) * slots // CHUNKS)
    inner(sx)
    x_arrive()
    fill_sides(sx, xw)
    outer(sx)

    def store_y(i, value):
        yw[:, pl.ds(reach + i * width, width)] = value

    summed_rows(prods, codes, row_tiles, store_y)
    y_start()

    fill_own(sp, pw)
    inner(sp)
    p_arrive()
    fill_sides(sp, pw)
    outer(sp)

    def store_q(i, value):
        q[:, pl.ds(i * width, width)] = value

    summed_rows(prods, codes, row_tiles, store_q)

    pl.semaphore_wait(middle, 2)
    greet(far, {"rows": layer_by(2 * near)})
    greet(far, {"rows": layer_by(-2 * near)})

    fill_own(sy, yw)
    inner(sy)

    def gram_of(right):
        left = jnp.concatenate([xw[:, own], yw[:, own], pw[:, own]], axis=0)
        return lax.dot_general(
            left, right, (((1,), (1,)), ((), ())), precision=lax.Precision.HIGHEST,
            preferred_element_type=F32,
        )

    gram = gram_of(
        jnp.concatenate(
            [xw[:, own], yw[:, own], pw[:, own], q[...], jnp.zeros((4 * channels, here), F32)],
            axis=0,
        )
    )
    y_arrive()
    fill_sides(sy, yw)
    outer(sy)

    def store_z(i, value):
        z[:, pl.ds(i * width, width)] = value

    summed_rows(prods, codes, row_tiles, store_z)
    gram = gram + gram_of(
        jnp.concatenate(
            [jnp.zeros((4 * channels, here), F32), z[...], jnp.zeros((3 * channels, here), F32)],
            axis=0,
        )
    )
    gram_x, gram_y, gram_p = (gram[i * channels : (i + 1) * channels] for i in range(3))
    lane = lax.broadcasted_iota(jnp.int32, (channels, 128), 1)
    first = jnp.where(lane < 5 * channels, gram_x, pltpu.roll(gram_p, 3 * channels, 1))
    half = channels // 2
    lane = lax.broadcasted_iota(jnp.int32, (half, 128), 1)
    second = jnp.where(
        jnp.logical_and(lane >= channels, lane < 5 * channels),
        gram_y[:half], pltpu.roll(gram_y[half:], 64, 1),
    )
    packed = jnp.concatenate([first, second], axis=0)
    rows_each = PACKED // members
    for i in range(members):
        parts[i] = packed[i * rows_each : (i + 1) * rows_each]

    def spread(offset, incoming=False):
        other, device = member_by(offset)
        slot = other if incoming else member
        return pltpu.make_async_remote_copy(
            src_ref=parts.at[other], dst_ref=arrived.at[slot], send_sem=send_a.at[other],
            recv_sem=recv_a.at[slot], device_id=device, device_id_type=MESH,
        )

    def over(k, incoming=False):
        other = layer_at(k)
        slot = other if incoming else layer
        return pltpu.make_async_remote_copy(
            src_ref=along.at[layer], dst_ref=along.at[slot], send_sem=send_b.at[other],
            recv_sem=recv_b.at[slot], device_id={"rows": other}, device_id_type=MESH,
        )

    def share(offset, incoming=False):
        other, device = member_by(offset)
        slot = other if incoming else member
        return pltpu.make_async_remote_copy(
            src_ref=gathered.at[member], dst_ref=gathered.at[slot], send_sem=send_c.at[other],
            recv_sem=recv_c.at[slot], device_id=device, device_id_type=MESH,
        )

    others = range(1, members)
    for i in others:
        spread(i).start()
    arrived[member] = parts[member]
    outs = [
        pltpu.make_async_copy(yw.at[:, own], y_any, out_sems.at[0]),
        pltpu.make_async_copy(z, z_any, out_sems.at[1]),
    ]
    for out in outs:
        out.start()
    pl.semaphore_wait(far, 2)
    for i in others:
        spread(i, True).wait_recv()
    along[layer] = jnp.sum(arrived[...], axis=0)
    each(depth - 1, lambda k: over(k).start())
    x_finish()
    p_finish()
    y_finish()
    for out in outs:
        out.wait()
    for i in others:
        spread(i).wait_send()
    each(depth - 1, lambda k: over(k, True).wait_recv())
    gathered[member] = jnp.sum(along[...], axis=0)
    for i in others:
        share(i).start()
    each(depth - 1, lambda k: over(k).wait_send())
    for i in others:
        share(i, True).wait_recv()
    total_ref[...] = gathered[...]
    for i in others:
        share(i).wait_send()


def eliminated(matrix):
    n, lanes = matrix.shape
    block = 16
    pieces = [matrix[i : i + block] for i in range(0, n, block)]
    done = []
    for b in range(n // block):
        rest = jnp.concatenate(pieces[b:], axis=0) if b < n // block - 1 else pieces[b]
        tall = rest.shape[0]
        row = lax.broadcasted_iota(jnp.int32, (tall, lanes), 0)
        columns = [
            jnp.broadcast_to(rest[:, b * block + j : b * block + j + 1], (tall, lanes))
            for j in range(block)
        ]
        pivots = jnp.ones((block, lanes), F32)
        for j in range(block):
            pivot = columns[j][j : j + 1]
            inverse = 1.0 / pivot
            pivots = jnp.where(row[:block] == j, pivot, pivots)
            below = jnp.where(row > j, columns[j], 0.0)
            rest = rest - below * (rest[j : j + 1] * inverse)
            for i in range(j + 1, block):
                columns[i] = columns[i] - below * (columns[i][j : j + 1] * inverse)
        pieces[b:] = [rest[i : i + block] for i in range(0, tall, block)]
        done.append(pieces[b] * lax.rsqrt(pivots))
    return jnp.concatenate(done, axis=0) if len(done) > 1 else done[0]


def precise(left, right, turned=False):
    return lax.dot_general(
        left, right, (((1,), (1 if turned else 0,)), ((), ())),
        precision=lax.Precision.HIGHEST, preferred_element_type=F32,
    )


def dense_kernel(
    vertex_total, total_ref, x_any, y_any, z_any, locked_any, w_any, image_any, ritz,
    xs, ys, zs, w, image, locked_s, sems,
):
    channels = xs.shape[0]
    loads = [
        pltpu.make_async_copy(source, target, sems.at[i])
        for i, (source, target) in enumerate(
            ((locked_any, locked_s), (x_any, xs), (y_any, ys), (z_any, zs))
        )
    ]
    for load in loads:
        load.start()
    packed = jnp.concatenate([total_ref[i] for i in range(total_ref.shape[0])], axis=0)
    first, folded = packed[:channels], packed[channels:]

    def part(v, i):
        return v[:, i * channels : (i + 1) * channels]

    xx, xy, xp, xq, xz, pp, pq, pz = (part(first, i) for i in range(8))
    second = jnp.concatenate([folded, pltpu.roll(folded, 64, 1)], axis=0)
    yy, yp = part(second, 1), part(second, 2)
    shape = (channels, channels)
    row = lax.broadcasted_iota(jnp.int32, shape, 0)
    column = lax.broadcasted_iota(jnp.int32, shape, 1)
    eye = jnp.where(row == column, 1.0, 0.0).astype(F32)
    yx = xy.T
    top = eye * (xy + 1e-06)
    below = eye * (xx + 1e-06)
    c_down = jnp.sum(top, axis=1, keepdims=True) / jnp.sum(below, axis=1, keepdims=True)
    c_along = jnp.sum(top, axis=0, keepdims=True) / jnp.sum(below, axis=0, keepdims=True)
    loads[0].wait()
    locked = locked_s[0]
    free_down = (lax.broadcasted_iota(jnp.int32, (channels, 1), 0) >= locked).astype(F32)
    free_along = (lax.broadcasted_iota(jnp.int32, (1, channels), 1) >= locked).astype(F32)
    scale = 1.0 / vertex_total
    frozen = eye * (1.0 - free_down)
    rx = free_down * (c_down * xx - yx)
    ry = free_down * (c_down * xy - yy)
    gram_w = free_along * (rx * c_along - ry) * scale + frozen
    inverse = eliminated(jnp.concatenate([gram_w, eye], axis=1))[:, channels:]

    lane = lax.broadcasted_iota(jnp.int32, first.shape, 1)
    rd = jnp.where(lane < channels, jnp.concatenate([rx] * 8, axis=1), free_down * (c_down * first - second))
    wd = precise(inverse, rd)
    wx, wy, wp, wq, wz = (part(wd, i) for i in range(5))
    px, py = xp.T, yp.T

    def against_r(vx, vy):
        return free_along * (vx * c_along - vy)

    def against_image(vx, vy, vz):
        return free_along * (c_along * (vx - vy) - vy + vz)

    stacked = jnp.concatenate(
        [against_r(wx, wy), against_image(xx, xy, xz), against_image(wx, wy, wz),
         against_image(px, py, pz)], axis=0,
    )
    stacked = precise(stacked, inverse, turned=True)
    ww, xaw, waw, paw = (stacked[i * channels : (i + 1) * channels] for i in range(4))

    for load in loads[1:]:
        load.wait()
    r = free_down * (c_down * xs[...] - ys[...])
    nr = free_down * (c_down * ys[...] - zs[...])
    w[...] = precise(inverse, r)
    image[...] = precise(inverse, r - nr)
    stores = [
        pltpu.make_async_copy(w, w_any, sems.at[4]),
        pltpu.make_async_copy(image, image_any, sems.at[5]),
    ]
    for store in stores:
        store.start()

    gram_b = jnp.concatenate(
        [
            jnp.concatenate([xx, wx.T, xp], axis=1) * scale,
            jnp.concatenate([wx * scale, ww * scale + frozen, wp * scale], axis=1),
            jnp.concatenate([px, wp.T, pp], axis=1) * scale,
        ], axis=0,
    )
    gram_a = jnp.concatenate(
        [
            jnp.concatenate([xx - xy, xaw, xp - xq], axis=1),
            jnp.concatenate([wx - wy, waw, wp - wq], axis=1),
            jnp.concatenate([px - py, paw, pp - pq], axis=1),
        ], axis=0,
    ) * scale
    n = 3 * channels
    big = (
        lax.broadcasted_iota(jnp.int32, (n, n), 0) == lax.broadcasted_iota(jnp.int32, (n, n), 1)
    ).astype(F32)
    lower = eliminated(jnp.concatenate([gram_b, big], axis=1))[:, n:]
    symmetric = 0.5 * (gram_a + gram_a.T)
    ritz[...] = precise(precise(lower, symmetric), lower, turned=True)
    for store in stores:
        store.wait()


def body(sizes, current_block, previous_block, adjacency_tiles, tile_rows, tile_cols, tile_count, locked):
    channels, here = current_block.shape
    slots, width, _ = adjacency_tiles.shape
    depth, cols, sub = sizes
    members = cols * sub
    rows_each = PACKED // members
    span = 2 * here // width
    vmem = pl.BlockSpec(memory_space=pltpu.VMEM)
    anywhere = pl.BlockSpec(memory_space=pl.ANY)
    dma = pltpu.SemaphoreType.DMA
    regular = pltpu.SemaphoreType.REGULAR
    i32 = jnp.int32

    def like(*shape):
        return jax.ShapeDtypeStruct(shape, F32)

    total, y, z = pl.pallas_call(
        functools.partial(main_kernel, sizes),
        name="main",
        out_shape=(like(members, rows_each, 128), like(channels, here), like(channels, here)),
        in_specs=[anywhere] * 6,
        out_specs=(vmem, anywhere, anywhere),
        scratch_shapes=[
            VMEM((channels, 2 * here), F32),
            VMEM((channels, 2 * here), F32),
            VMEM((channels, 2 * here), F32),
            VMEM((span, 2 * channels, width), BF16),
            VMEM((span, 2 * channels, width), BF16),
            VMEM((span, 2 * channels, width), BF16),
            VMEM((slots, width, width), F32),
            VMEM((slots, width, 2 * width), BF16),
            VMEM((slots, channels, width), F32),
            VMEM((channels, here), F32),
            VMEM((channels, here), F32),
            VMEM((members, rows_each, 128), F32),
            VMEM((members, rows_each, 128), F32),
            VMEM((depth, rows_each, 128), F32),
            VMEM((members, rows_each, 128), F32),
            pltpu.SMEM((slots,), i32), pltpu.SMEM((slots,), i32),
            pltpu.SMEM((1,), i32), pltpu.SMEM((slots,), i32),
            dma((5,)), dma((CHUNKS,)), dma((6,)), dma((6,)),
            dma((members,)), dma((members,)),
            dma((depth,)), dma((depth,)),
            dma((members,)), dma((members,)),
            dma((2,)), regular, regular,
        ],
        compiler_params=pltpu.CompilerParams(collective_id=0, has_side_effects=True),
    )(current_block, previous_block, adjacency_tiles, tile_rows, tile_cols, tile_count)
    return pl.pallas_call(
        functools.partial(dense_kernel, float(here * depth * members)),
        name="dense",
        out_shape=(like(channels, here), like(channels, here), like(3 * channels, 3 * channels)),
        in_specs=[vmem] + [anywhere] * 4,
        out_specs=(anywhere, anywhere, vmem),
        scratch_shapes=[VMEM((channels, here), F32)] * 5
        + [pltpu.SMEM((1,), i32), dma((6,))],
    )(total, current_block, y, z, locked)


def solution(mesh):
    sizes = tuple(mesh.shape[a] for a in VERTEX_AXES)
    everywhere = ("graphs", "rows", "cols", "sub")
    in_specs = (
        P(None, everywhere),
        P(None, everywhere),
        P(everywhere, None, None),
        P(everywhere),
        P(everywhere),
        P(everywhere),
        P("graphs"),
    )
    out_specs = (P(None, everywhere), P(None, everywhere), P("graphs", None))
    return jax.shard_map(
        functools.partial(body, sizes), mesh=mesh, in_specs=in_specs, out_specs=out_specs,
        check_vma=False,
    )
```

time: 363 us -> 83 us (0.23)
  blocking collectives: 262 us -> 0 us
  Pallas kernels: 0 us -> 80.9 us
  starting transfers between devices: 50.2 us -> 0 us
  other arithmetic: 21 us -> 0 us
  matrix products: 15.9 us -> 0 us
  local copies, waits for them, and re-layouts: 9.13 us -> 0 us
    psum x9 -> x0, blocking collectives: 262 us -> none  [one_axis_at_a_time(): value = lax.psum(value, axis)]
    pallas_call x0 -> x2, Pallas kernels: none -> 80.9 us  [the longest x1 76 us: body(): pl.pallas_call(functools.partial(main_kernel, sizes), name='main', out_sh...]
    ppermute x4 -> x0, starting transfers between devices: 50.2 us -> none  [the longest x2 42.7 us: extended(): lax.ppermute(initial, axis, [(b, a) for a, b in up])]
    dot_general x7 -> x0, matrix products: 13.6 us -> none  [the longest x2 7.81 us: operate(): jnp.einsum('cta,tab->ctb', gathered, adjacency_tiles, precision=lax.Preci...]
    another operation x10 -> x0, other arithmetic: 13.4 us -> none  [the longest x4 6.2 us: solve_lower(): lax.linalg.triangular_solve(factor, values, left_side=True, lower=True)]
    gather x2 -> x0, local copies, waits for them, and re-layouts: 4.78 us -> none  [operate(): gathered = jnp.take(column_blocks, column_position, axis=1)]
  transfers between devices with their start and end apart: 4 -> 0, of which waited for: 1 -> 0; matrix products, arithmetic and copies ran while one was open for 1% -> 0% of each run, Pallas kernels for 0% -> 0%
where the time goes in v2:
time: 83 us; the launch traced here: 82.8 us
  Pallas kernels  80.9 us (97%)
  between operations  1.93 us (2%)
    pallas_call x1, Pallas kernels, body(): pl.pallas_call(functools.partial(main_kernel, sizes), name='main', out_sh...  76 us
    pallas_call x1, Pallas kernels, body(): pl.pallas_call(functools.partial(dense_kernel, float(here * depth * membe...  4.89 us

profile of v2, /device:TPU:33, one launch (start us, length us, event | category | flops | bytes accessed | tf_op | source)
XLA Modules:
  0.0 82.8 jit_solution(12800256645839892742)
XLA Ops:
  1.9 76.0 %main.1 = (f32[8,3,128]{2,1,0:T(4,128)}, f32[16,2048]{1,0:T(8,128)}, f32[16,2048]{1,0:T(8,128)}) custom-call(f32[16,2048]{1,0:T(8,128)} %x_any.3, f32[16,2048]{1,0:T(8,128)} %p_any.1, f32[48,128,128]{2,1,0:T(8,128)} %tiles_any.1, s32[48]{0:T(128)} %rows_any.1, s32[48]{0:T(128)} %cols_any.1, s32[1]{0:T(128)S(6)} %copy.10.count_any), custom_call_target="tpu_custom_call" | custom-call | tf_op jit(solution)/shard_map/main/pallas_call | solution.py:546
  77.9 4.9 %dense.1 = (f32[16,2048]{1,0:T(8,128)}, f32[16,2048]{1,0:T(8,128)}, f32[48,48]{1,0:T(8,128)}) custom-call(f32[8,3,128]{2,1,0:T(4,128)} %get-tuple-element.6.total_ref, f32[16,2048]{1,0:T(8,128)} %x_any.3, f32[16,2048]{1,0:T(8,128)} %get-tuple-element.7.y_any, f32[16,2048]{1,0:T(8,128)} %get-tuple-element.8.z_any, s32[1]{0:T(128)S(6)} %copy.11.locked_any), custom_call_target="tpu_custom_call" | custom-call | tf_op jit(solution)/shard_map/dense/pallas_call | solution.py:578

commit v3 on v2

--- a/solution.py
+++ b/solution.py
@@ -90,9 +90,9 @@
 
 def device_at(position, sizes):
     return {
-        "rows": position // (sizes[1] * sizes[2]),
-        "cols": (position // sizes[2]) % sizes[1],
-        "sub": position % sizes[2],
+        "rows": lax.div(position, sizes[1] * sizes[2]),
+        "cols": lax.rem(lax.div(position, sizes[2]), sizes[1]),
+        "sub": lax.rem(position, sizes[2]),
     }
 
 
@@ -100,7 +100,7 @@
     sizes, x_any, p_any, tiles_any, rows_any, cols_any, count_any, total_ref, y_any, z_any,
     xw, pw, yw, sx, sp, sy, tiles, pairs, prods, q, z, parts, arrived, along, gathered,
     rows_s, cols_s, count_s, codes, load_sems, tile_sems, halo_send, halo_recv,
-    send_a, recv_a, send_b, recv_b, send_c, recv_c, out_sems, middle, far,
+    send_a, recv_a, send_b, recv_b, send_c, recv_c, out_sems, from_low, from_high, gram_s,
 ):
     channels, here = q.shape
     slots, width, _ = tiles.shape
@@ -114,7 +114,10 @@
     base = me * row_tiles
     layer = lax.axis_index("rows")
     member = lax.axis_index("cols") * sub + lax.axis_index("sub")
-    near = depth // 8
+    near = max(1, depth // 16)
+    stages = [near]
+    while 2 * stages[-1] < depth // 2:
+        stages.append(2 * stages[-1])
     own = pl.ds(reach, here)
     low_side, high_side = pl.ds(0, reach), pl.ds(reach + here, reach)
 
@@ -124,13 +127,12 @@
         return jnp.where(other < 0, other + depth, other)
 
     def layer_at(k):
-        half = (k + 1) // 2
-        return layer_by(depth // 2 + jnp.where(k % 2 == 1, half, -half))
+        return layer_by(k + 1)
 
     def member_by(offset):
         other = member + offset
         other = jnp.where(other >= members, other - members, other)
-        return other, {"cols": other // sub, "sub": other % sub}
+        return other, {"cols": lax.div(other, sub), "sub": lax.rem(other, sub)}
 
     def each(n, act):
         def step(k, carry):
@@ -139,13 +141,26 @@
 
         lax.fori_loop(0, n, step, 0)
 
+    def tell(stage):
+        greet(from_low.at[stage], {"rows": layer_by(stages[stage])})
+        greet(from_high.at[stage], {"rows": layer_by(-stages[stage])})
+
+    def hear(stage):
+        pl.semaphore_wait(from_low.at[stage], 1)
+        pl.semaphore_wait(from_high.at[stage], 1)
+
+    last = len(stages) - 1
     barrier = pltpu.get_barrier_semaphore()
 
     def greet(semaphore, device):
         pl.semaphore_signal(semaphore, inc=1, device_id=device, device_id_type=MESH)
 
     has_low, has_high = me > 0, me < total - 1
-    low, high = device_at(me - 1, sizes), device_at(me + 1, sizes)
+    low = device_at(jnp.maximum(me - 1, 0), sizes)
+    high = device_at(jnp.minimum(me + 1, total - 1), sizes)
+
+    load_x = pltpu.make_async_copy(x_any, xw.at[:, own], load_sems.at[0])
+    load_x.start()
 
     @pl.when(has_low)
     def _():
@@ -155,7 +170,11 @@
     def _():
         greet(barrier, high)
 
-    load_x = pltpu.make_async_copy(x_any, xw.at[:, own], load_sems.at[0])
+    for offset in range(1, members):
+        greet(barrier, member_by(offset)[1])
+    for offset in range(1, near + 1):
+        greet(barrier, {"rows": layer_by(offset)})
+        greet(barrier, {"rows": layer_by(-offset)})
     load_p = pltpu.make_async_copy(p_any, pw.at[:, own], load_sems.at[1])
     small = [
         pltpu.make_async_copy(source, target, load_sems.at[2 + i])
@@ -164,13 +183,8 @@
         )
     ]
     loads = tile_copies(tiles_any, tiles, tile_sems)
-    for load in [load_x, load_p, *small, *loads]:
+    for load in [load_p, *small, *loads]:
         load.start()
-    for offset in range(1, members):
-        greet(barrier, member_by(offset)[1])
-    for offset in range(1, near + 1):
-        greet(barrier, {"rows": layer_by(offset)})
-        greet(barrier, {"rows": layer_by(-offset)})
     pl.semaphore_wait(
         barrier,
         has_low.astype(jnp.int32) + has_high.astype(jnp.int32) + (members - 1 + 2 * near),
@@ -224,8 +238,7 @@
     x_start()
     load_p.wait()
     p_start()
-    greet(middle, {"rows": layer_by(near)})
-    greet(middle, {"rows": layer_by(-near)})
+    tell(0)
 
     @pl.when(jnp.logical_not(has_low))
     def _():
@@ -267,6 +280,9 @@
         load.wait()
         split_tiles(tiles, pairs, i * slots // CHUNKS, (i + 1) * slots // CHUNKS)
     inner(sx)
+    for stage in range(last - 1):
+        hear(stage)
+        tell(stage + 1)
     x_arrive()
     fill_sides(sx, xw)
     outer(sx)
@@ -288,9 +304,8 @@
 
     summed_rows(prods, codes, row_tiles, store_q)
 
-    pl.semaphore_wait(middle, 2)
-    greet(far, {"rows": layer_by(2 * near)})
-    greet(far, {"rows": layer_by(-2 * near)})
+    hear(last - 1)
+    tell(last)
 
     fill_own(sy, yw)
     inner(sy)
@@ -302,7 +317,7 @@
             preferred_element_type=F32,
         )
 
-    gram = gram_of(
+    gram_s[...] = gram_of(
         jnp.concatenate(
             [xw[:, own], yw[:, own], pw[:, own], q[...], jnp.zeros((4 * channels, here), F32)],
             axis=0,
@@ -316,12 +331,9 @@
         z[:, pl.ds(i * width, width)] = value
 
     summed_rows(prods, codes, row_tiles, store_z)
-    gram = gram + gram_of(
-        jnp.concatenate(
-            [jnp.zeros((4 * channels, here), F32), z[...], jnp.zeros((3 * channels, here), F32)],
-            axis=0,
-        )
-    )
+    with_z = gram_of(z[...])
+    with_z = jnp.concatenate([with_z, jnp.zeros((3 * channels, 128 - channels), F32)], axis=1)
+    gram = gram_s[...] + pltpu.roll(with_z, 4 * channels, 1)
     gram_x, gram_y, gram_p = (gram[i * channels : (i + 1) * channels] for i in range(3))
     lane = lax.broadcasted_iota(jnp.int32, (channels, 128), 1)
     first = jnp.where(lane < 5 * channels, gram_x, pltpu.roll(gram_p, 3 * channels, 1))
@@ -370,11 +382,18 @@
     ]
     for out in outs:
         out.start()
-    pl.semaphore_wait(far, 2)
     for i in others:
         spread(i, True).wait_recv()
     along[layer] = jnp.sum(arrived[...], axis=0)
-    each(depth - 1, lambda k: over(k).start())
+    pl.semaphore_wait(from_low.at[last], 1)
+    for k in range(depth // 2, depth - stages[last]):
+        over(k - 1).start()
+    pl.semaphore_wait(from_high.at[last], 1)
+    for k in range(depth // 2 - 1, 0, -1):
+        over(k - 1).start()
+        if k < stages[last]:
+            over(depth - k - 1).start()
+    over(depth - stages[last] - 1).start()
     x_finish()
     p_finish()
     y_finish()
@@ -535,7 +554,7 @@
     rows_each = PACKED // members
     span = 2 * here // width
     vmem = pl.BlockSpec(memory_space=pltpu.VMEM)
-    anywhere = pl.BlockSpec(memory_space=pl.ANY)
+    anywhere = pl.BlockSpec(memory_space=pltpu.HBM)
     dma = pltpu.SemaphoreType.DMA
     regular = pltpu.SemaphoreType.REGULAR
     i32 = jnp.int32
@@ -571,7 +590,7 @@
             dma((members,)), dma((members,)),
             dma((depth,)), dma((depth,)),
             dma((members,)), dma((members,)),
-            dma((2,)), regular, regular,
+            dma((2,)), regular((4,)), regular((4,)), VMEM((3 * channels, 128), F32),
         ],
         compiler_params=pltpu.CompilerParams(collective_id=0, has_side_effects=True),
     )(current_block, previous_block, adjacency_tiles, tile_rows, tile_cols, tile_count)

time: 83 us -> 80.9 us (0.975)
  Pallas kernels: 80.9 us -> 78.8 us
    pallas_call x1, Pallas kernels: 76 us -> 73.9 us  [body(): pl.pallas_call(functools.partial(main_kernel, sizes), name='main', out_sh...]
where the time goes in v3:
time: 80.9 us; the launch traced here: 80.7 us
  Pallas kernels  78.8 us (97%)
  between operations  1.93 us (2%)
    pallas_call x1, Pallas kernels, body(): pl.pallas_call(functools.partial(main_kernel, sizes), name='main', out_sh...  73.9 us
    pallas_call x1, Pallas kernels, body(): pl.pallas_call(functools.partial(dense_kernel, float(here * depth * membe...  4.89 us

profile of v3, /device:TPU:33, one launch (start us, length us, event | category | flops | bytes accessed | tf_op | source)
XLA Modules:
  0.0 80.7 jit_solution(14460606895002681828)
XLA Ops:
  1.9 73.9 %main.1 = (f32[8,3,128]{2,1,0:T(4,128)}, f32[16,2048]{1,0:T(8,128)}, f32[16,2048]{1,0:T(8,128)}) custom-call(f32[16,2048]{1,0:T(8,128)} %x_any.3, f32[16,2048]{1,0:T(8,128)} %p_any.1, f32[48,128,128]{2,1,0:T(8,128)} %tiles_any.1, s32[48]{0:T(128)} %rows_any.1, s32[48]{0:T(128)} %cols_any.1, s32[1]{0:T(128)S(6)} %copy.10.count_any), custom_call_target="tpu_custom_call" | custom-call | tf_op jit(solution)/shard_map/main/pallas_call | solution.py:565
  75.8 4.9 %dense.1 = (f32[16,2048]{1,0:T(8,128)}, f32[16,2048]{1,0:T(8,128)}, f32[48,48]{1,0:T(8,128)}) custom-call(f32[8,3,128]{2,1,0:T(4,128)} %get-tuple-element.6.total_ref, f32[16,2048]{1,0:T(8,128)} %x_any.3, f32[16,2048]{1,0:T(8,128)} %get-tuple-element.7.y_any, f32[16,2048]{1,0:T(8,128)} %get-tuple-element.8.z_any, s32[1]{0:T(128)S(6)} %copy.11.locked_any), custom_call_target="tpu_custom_call" | custom-call | tf_op jit(solution)/shard_map/dense/pallas_call | solution.py:597

commit v4 on v3

--- a/solution.py
+++ b/solution.py
@@ -65,7 +65,7 @@
     lax.fori_loop(first // GROUP, last // GROUP, step, 0)
 
 
-def summed_rows(prods, codes, row_tiles, store):
+def summed_rows(prods, codes, row_tiles, store, after=None):
     slots, channels, width = prods.shape
     size = row_tiles // 2
     for block in range(2):
@@ -81,6 +81,8 @@
         )
         for i, s in zip(mine, sums):
             store(i, s)
+        if after is not None:
+            after[block]()
 
 
 def place(sizes):
@@ -201,11 +203,12 @@
         down = remote(pl.ds(reach, reach), high_side, 2 * n, low)
         up = remote(pl.ds(here, reach), low_side, 2 * n + 1, high)
 
-        def start():
+        def start_down():
             @pl.when(has_low)
             def _():
                 down.start()
 
+        def start_up():
             @pl.when(has_high)
             def _():
                 up.start()
@@ -228,16 +231,18 @@
             def _():
                 up.wait_send()
 
-        return start, arrive, finish
+        return (start_down, start_up), arrive, finish
 
     x_start, x_arrive, x_finish = halo(xw, 0)
     p_start, p_arrive, p_finish = halo(pw, 1)
     y_start, y_arrive, y_finish = halo(yw, 2)
 
     load_x.wait()
-    x_start()
+    for start in x_start:
+        start()
     load_p.wait()
-    p_start()
+    for start in p_start:
+        start()
     tell(0)
 
     @pl.when(jnp.logical_not(has_low))
@@ -290,8 +295,7 @@
     def store_y(i, value):
         yw[:, pl.ds(reach + i * width, width)] = value
 
-    summed_rows(prods, codes, row_tiles, store_y)
-    y_start()
+    summed_rows(prods, codes, row_tiles, store_y, y_start)
 
     fill_own(sp, pw)
     inner(sp)
@@ -447,6 +451,14 @@
     )
 
 
+def three_products(left, right):
+    rows = left.shape[0]
+    high, low = halves(left)
+    top, bottom = halves(right)
+    out = jnp.dot(jnp.concatenate([high, low], axis=0), top, preferred_element_type=F32)
+    return out[:rows] + (out[rows:] + jnp.dot(high, bottom, preferred_element_type=F32))
+
+
 def dense_kernel(
     vertex_total, total_ref, x_any, y_any, z_any, locked_any, w_any, image_any, ritz,
     xs, ys, zs, w, image, locked_s, sems,
@@ -512,8 +524,8 @@
         load.wait()
     r = free_down * (c_down * xs[...] - ys[...])
     nr = free_down * (c_down * ys[...] - zs[...])
-    w[...] = precise(inverse, r)
-    image[...] = precise(inverse, r - nr)
+    w[...] = three_products(inverse, r)
+    image[...] = three_products(inverse, r - nr)
     stores = [
         pltpu.make_async_copy(w, w_any, sems.at[4]),
         pltpu.make_async_copy(image, image_any, sems.at[5]),
@@ -565,7 +577,7 @@
     total, y, z = pl.pallas_call(
         functools.partial(main_kernel, sizes),
         name="main",
-        out_shape=(like(members, rows_each, 128), like(channels, here), like(channels, here)),
+        out_shape=(pltpu.VMEM((members, rows_each, 128), F32), like(channels, here), like(channels, here)),
         in_specs=[anywhere] * 6,
         out_specs=(vmem, anywhere, anywhere),
         scratch_shapes=[
@@ -602,7 +614,7 @@
         out_specs=(anywhere, anywhere, vmem),
         scratch_shapes=[VMEM((channels, here), F32)] * 5
         + [pltpu.SMEM((1,), i32), dma((6,))],
-    )(total, current_block, y, z, locked)
+    )(pltpu.with_memory_space_constraint(total, pltpu.VMEM), current_block, y, z, locked)
 
 
 def solution(mesh):

time: 80.9 us -> 79.3 us (0.980)
  Pallas kernels: 78.8 us -> 77.3 us
    pallas_call x1, Pallas kernels: 4.89 us -> 3.99 us  [body(): pl.pallas_call(functools.partial(dense_kernel, float(here * depth * membe...]
where the time goes in v4:
time: 79.3 us; the launch traced here: 79.2 us
  Pallas kernels  77.3 us (97%)
  between operations  1.93 us (2%)
    pallas_call x1, Pallas kernels, body(): pl.pallas_call(functools.partial(main_kernel, sizes), name='main', out_sh...  73.3 us
    pallas_call x1, Pallas kernels, body(): pl.pallas_call(functools.partial(dense_kernel, float(here * depth * membe...  3.99 us

profile of v4, /device:TPU:33, one launch (start us, length us, event | category | flops | bytes accessed | tf_op | source)
XLA Modules:
  0.0 79.2 jit_solution(16541011408555073356)
XLA Ops:
  1.9 73.3 %main.1 = (f32[8,3,128]{2,1,0:T(4,128)S(1)}, f32[16,2048]{1,0:T(8,128)}, f32[16,2048]{1,0:T(8,128)}) custom-call(f32[16,2048]{1,0:T(8,128)} %x_any.3, f32[16,2048]{1,0:T(8,128)} %p_any.1, f32[48,128,128]{2,1,0:T(8,128)} %tiles_any.1, s32[48]{0:T(128)} %rows_any.1, s32[48]{0:T(128)} %cols_any.1, s32[1]{0:T(128)S(6)} %copy.10.count_any), custom_call_target="tpu_custom_call" | custom-call | tf_op jit(solution)/shard_map/main/pallas_call | solution.py:577
  75.2 4.0 %dense.1 = (f32[16,2048]{1,0:T(8,128)}, f32[16,2048]{1,0:T(8,128)}, f32[48,48]{1,0:T(8,128)}) custom-call(f32[8,3,128]{2,1,0:T(4,128)S(1)} %get-tuple-element.6.total_ref, f32[16,2048]{1,0:T(8,128)} %x_any.3, f32[16,2048]{1,0:T(8,128)} %get-tuple-element.7.y_any, f32[16,2048]{1,0:T(8,128)} %get-tuple-element.8.z_any, s32[1]{0:T(128)S(6)} %copy.11.locked_any), custom_call_target="tpu_custom_call" | custom-call | tf_op jit(solution)/shard_map/dense/pallas_call | solution.py:609

commit v5 on v4

--- a/solution.py
+++ b/solution.py
@@ -102,7 +102,7 @@
     sizes, x_any, p_any, tiles_any, rows_any, cols_any, count_any, total_ref, y_any, z_any,
     xw, pw, yw, sx, sp, sy, tiles, pairs, prods, q, z, parts, arrived, along, gathered,
     rows_s, cols_s, count_s, codes, load_sems, tile_sems, halo_send, halo_recv,
-    send_a, recv_a, send_b, recv_b, send_c, recv_c, out_sems, from_low, from_high, gram_s,
+    send_a, recv_a, send_b, recv_b, send_c, recv_c, out_sems, from_low, from_high, ring_low, ring_high, gram_s,
 ):
     channels, here = q.shape
     slots, width, _ = tiles.shape
@@ -134,6 +134,7 @@
     def member_by(offset):
         other = member + offset
         other = jnp.where(other >= members, other - members, other)
+        other = jnp.where(other < 0, other + members, other)
         return other, {"cols": lax.div(other, sub), "sub": lax.rem(other, sub)}
 
     def each(n, act):
@@ -151,6 +152,18 @@
         pl.semaphore_wait(from_low.at[stage], 1)
         pl.semaphore_wait(from_high.at[stage], 1)
 
+    rings = []
+    while members > 1 and 2 ** len(rings) < members // 2:
+        rings.append(2 ** len(rings))
+
+    def tell_members(stage):
+        greet(ring_low.at[stage], member_by(rings[stage])[1])
+        greet(ring_high.at[stage], member_by(-rings[stage])[1])
+
+    def hear_members(stage):
+        pl.semaphore_wait(ring_low.at[stage], 1)
+        pl.semaphore_wait(ring_high.at[stage], 1)
+
     last = len(stages) - 1
     barrier = pltpu.get_barrier_semaphore()
 
@@ -172,7 +185,8 @@
     def _():
         greet(barrier, high)
 
-    for offset in range(1, members):
+    adjacent = 2 if members > 1 else 0
+    for offset in (1, -1)[:adjacent]:
         greet(barrier, member_by(offset)[1])
     for offset in range(1, near + 1):
         greet(barrier, {"rows": layer_by(offset)})
@@ -189,7 +203,7 @@
         load.start()
     pl.semaphore_wait(
         barrier,
-        has_low.astype(jnp.int32) + has_high.astype(jnp.int32) + (members - 1 + 2 * near),
+        has_low.astype(jnp.int32) + has_high.astype(jnp.int32) + (adjacent + 2 * near),
     )
 
     def halo(wide, n):
@@ -237,6 +251,8 @@
     p_start, p_arrive, p_finish = halo(pw, 1)
     y_start, y_arrive, y_finish = halo(yw, 2)
 
+    if rings:
+        tell_members(0)
     load_x.wait()
     for start in x_start:
         start()
@@ -285,6 +301,9 @@
         load.wait()
         split_tiles(tiles, pairs, i * slots // CHUNKS, (i + 1) * slots // CHUNKS)
     inner(sx)
+    for stage in range(1, len(rings)):
+        hear_members(stage - 1)
+        tell_members(stage)
     for stage in range(last - 1):
         hear(stage)
         tell(stage + 1)
@@ -377,6 +396,8 @@
         )
 
     others = range(1, members)
+    if rings:
+        hear_members(len(rings) - 1)
     for i in others:
         spread(i).start()
     arrived[member] = parts[member]
@@ -526,13 +547,6 @@
     nr = free_down * (c_down * ys[...] - zs[...])
     w[...] = three_products(inverse, r)
     image[...] = three_products(inverse, r - nr)
-    stores = [
-        pltpu.make_async_copy(w, w_any, sems.at[4]),
-        pltpu.make_async_copy(image, image_any, sems.at[5]),
-    ]
-    for store in stores:
-        store.start()
-
     gram_b = jnp.concatenate(
         [
             jnp.concatenate([xx, wx.T, xp], axis=1) * scale,
@@ -552,6 +566,13 @@
         lax.broadcasted_iota(jnp.int32, (n, n), 0) == lax.broadcasted_iota(jnp.int32, (n, n), 1)
     ).astype(F32)
     lower = eliminated(jnp.concatenate([gram_b, big], axis=1))[:, n:]
+    stores = [
+        pltpu.make_async_copy(w, w_any, sems.at[4]),
+        pltpu.make_async_copy(image, image_any, sems.at[5]),
+    ]
+    for store in stores:
+        store.start()
+
     symmetric = 0.5 * (gram_a + gram_a.T)
     ritz[...] = precise(precise(lower, symmetric), lower, turned=True)
     for store in stores:
@@ -602,7 +623,7 @@
             dma((members,)), dma((members,)),
             dma((depth,)), dma((depth,)),
             dma((members,)), dma((members,)),
-            dma((2,)), regular((4,)), regular((4,)), VMEM((3 * channels, 128), F32),
+            dma((2,)), regular((4,)), regular((4,)), regular((4,)), regular((4,)), VMEM((3 * channels, 128), F32),
         ],
         compiler_params=pltpu.CompilerParams(collective_id=0, has_side_effects=True),
     )(current_block, previous_block, adjacency_tiles, tile_rows, tile_cols, tile_count)

time: 79.3 us -> 79.3 us (level)
  no operation moved by 1% of the time
where the time goes in v5:
time: 79.3 us; the launch traced here: 79.2 us
  Pallas kernels  77.3 us (97%)
  between operations  1.93 us (2%)
    pallas_call x1, Pallas kernels, body(): pl.pallas_call(functools.partial(main_kernel, sizes), name='main', out_sh...  73.3 us
    pallas_call x1, Pallas kernels, body(): pl.pallas_call(functools.partial(dense_kernel, float(here * depth * membe...  3.99 us

profile of v5, /device:TPU:33, one launch (start us, length us, event | category | flops | bytes accessed | tf_op | source)
XLA Modules:
  0.0 79.2 jit_solution(9947188884640336753)
XLA Ops:
  1.9 73.3 %main.1 = (f32[8,3,128]{2,1,0:T(4,128)S(1)}, f32[16,2048]{1,0:T(8,128)}, f32[16,2048]{1,0:T(8,128)}) custom-call(f32[16,2048]{1,0:T(8,128)} %x_any.3, f32[16,2048]{1,0:T(8,128)} %p_any.1, f32[48,128,128]{2,1,0:T(8,128)} %tiles_any.1, s32[48]{0:T(128)} %rows_any.1, s32[48]{0:T(128)} %cols_any.1, s32[1]{0:T(128)S(6)} %copy.10.count_any), custom_call_target="tpu_custom_call" | custom-call | tf_op jit(solution)/shard_map/main/pallas_call | solution.py:598
  75.2 4.0 %dense.1 = (f32[16,2048]{1,0:T(8,128)}, f32[16,2048]{1,0:T(8,128)}, f32[48,48]{1,0:T(8,128)}) custom-call(f32[8,3,128]{2,1,0:T(4,128)S(1)} %get-tuple-element.6.total_ref, f32[16,2048]{1,0:T(8,128)} %x_any.3, f32[16,2048]{1,0:T(8,128)} %get-tuple-element.7.y_any, f32[16,2048]{1,0:T(8,128)} %get-tuple-element.8.z_any, s32[1]{0:T(128)S(6)} %copy.11.locked_any), custom_call_target="tpu_custom_call" | custom-call | tf_op jit(solution)/shard_map/dense/pallas_call | solution.py:630

commit v6 on v5

--- a/solution.py
+++ b/solution.py
@@ -327,11 +327,10 @@
 
     summed_rows(prods, codes, row_tiles, store_q)
 
+    fill_own(sy, yw)
+    inner(sy)
     hear(last - 1)
     tell(last)
-
-    fill_own(sy, yw)
-    inner(sy)
 
     def gram_of(right):
         left = jnp.concatenate([xw[:, own], yw[:, own], pw[:, own]], axis=0)

time: 79.3 us -> 79.3 us (level)
  no operation moved by 1% of the time
where the time goes in v6:
time: 79.3 us; the launch traced here: 79.2 us
  Pallas kernels  77.3 us (97%)
  between operations  1.93 us (2%)
    pallas_call x1, Pallas kernels, body(): pl.pallas_call(functools.partial(main_kernel, sizes), name='main', out_sh...  73.3 us
    pallas_call x1, Pallas kernels, body(): pl.pallas_call(functools.partial(dense_kernel, float(here * depth * membe...  3.99 us

profile of v6, /device:TPU:33, one launch (start us, length us, event | category | flops | bytes accessed | tf_op | source)
XLA Modules:
  0.0 79.2 jit_solution(6268234068147069195)
XLA Ops:
  1.9 73.3 %main.1 = (f32[8,3,128]{2,1,0:T(4,128)S(1)}, f32[16,2048]{1,0:T(8,128)}, f32[16,2048]{1,0:T(8,128)}) custom-call(f32[16,2048]{1,0:T(8,128)} %x_any.3, f32[16,2048]{1,0:T(8,128)} %p_any.1, f32[48,128,128]{2,1,0:T(8,128)} %tiles_any.1, s32[48]{0:T(128)} %rows_any.1, s32[48]{0:T(128)} %cols_any.1, s32[1]{0:T(128)S(6)} %copy.10.count_any), custom_call_target="tpu_custom_call" | custom-call | tf_op jit(solution)/shard_map/main/pallas_call | solution.py:597
  75.2 4.0 %dense.1 = (f32[16,2048]{1,0:T(8,128)}, f32[16,2048]{1,0:T(8,128)}, f32[48,48]{1,0:T(8,128)}) custom-call(f32[8,3,128]{2,1,0:T(4,128)S(1)} %get-tuple-element.6.total_ref, f32[16,2048]{1,0:T(8,128)} %x_any.3, f32[16,2048]{1,0:T(8,128)} %get-tuple-element.7.y_any, f32[16,2048]{1,0:T(8,128)} %get-tuple-element.8.z_any, s32[1]{0:T(128)S(6)} %copy.11.locked_any), custom_call_target="tpu_custom_call" | custom-call | tf_op jit(solution)/shard_map/dense/pallas_call | solution.py:629
